TPU v7x, 32 devices: a whole 2x2x4 slice. The times are simulated.
32 devices in a mesh: seq: 16 (over z, y, x), mp: 2 (over core).
Axes of the slice: x: 2, y: 2, z: 4, core: 2. Of those that a mesh axis runs over, the one named last changes fastest.
Arguments:
- encoded: bfloat16 [4096, 1152], P('seq'), may hold values from -6 to 6
- frame_tokens: int32 [16, 2], P('seq'), may hold values from 1 to 196, 256 in all within a row
- slot_owner: int32 [32], replicated, may hold values from 0 to 15, as said below
- w_in: bfloat16 [1152, 3584], P('seq', 'mp'), may hold values from -0.1875 to 0.1875
- b_in: bfloat16 [3584], P('mp'), may hold values from -3 to 3
- w_out: bfloat16 [3584, 3584], P('seq', 'mp'), may hold values from -0.09375 to 0.09375
- b_out: bfloat16 [3584], P('mp'), may hold values from -6.4 to 6.4
- norm_gain: bfloat16 [3584], replicated, may hold values from 0.5 to 1.5
- w_key: bfloat16 [3584, 512], P('seq', 'mp'), may hold values from -0.09375 to 0.09375
- b_key: bfloat16 [512], P('mp'), may hold values from -3 to 3
- w_value: bfloat16 [3584, 512], P('seq', 'mp'), may hold values from -0.09375 to 0.09375
- b_value: bfloat16 [512], P('mp'), may hold values from -3 to 3
Outputs:
- keys: bfloat16 [4096, 512], P('seq', 'mp')
- values: bfloat16 [4096, 512], P('seq', 'mp')
Inputs may be any that keep to these rules, and one draw needn't show every extreme that they name: `slot_owner`: each shard index 0 to 15 appears exactly twice. `frame_tokens`: each row sums to 256.
All inputs are finite; a program needn't handle non-finite values.
Results may differ from a plain program's by a relative error of at most 0.01.
Values may be sent and summed in bfloat16 or wider, within the bound.
A program may use at most 128 MiB of HBM per device.

v0:
```python
import jax
import jax.numpy as jnp
from jax import lax
from jax.sharding import PartitionSpec as P

D = 3584
HEAD = 128
TSEC = 16


norm_eps = 1e-06
rope_base = 1000000.0


def rotate(linear, frame_ids, offsets):
    pairs = HEAD // 2
    pair_index = jnp.arange(pairs)
    inverse = jnp.power(jnp.float32(rope_base), -2.0 * pair_index.astype(jnp.float32) / HEAD)
    chosen = jnp.where(pair_index[None, :] < TSEC, frame_ids[:, None], offsets[:, None]).astype(
        jnp.float32
    )
    angles = chosen * inverse[None, :]
    cosine = jnp.cos(angles)[:, None, :]
    sine = jnp.sin(angles)[:, None, :]
    shaped = linear.reshape(linear.shape[0], -1, HEAD)
    first_half = shaped[..., :pairs]
    second_half = shaped[..., pairs:]
    turned = jnp.concatenate(
        [first_half * cosine - second_half * sine, second_half * cosine + first_half * sine],
        axis=-1,
    )
    return turned.reshape(linear.shape)


def shards(
    encoded,
    frame_tokens,
    slot_owner,
    w_in,
    b_in,
    w_out,
    b_out,
    norm_gain,
    w_key,
    b_key,
    w_value,
    b_value,
):
    seq_count = lax.axis_size("seq")
    own_index = lax.axis_index("seq")
    tok_rows = encoded.shape[0]
    round_span = 2 * seq_count
    rounds = tok_rows // round_span
    frames_here = frame_tokens.shape[1]
    slot_order = jnp.argsort(slot_owner, stable=True)
    pick_rows = (
        jnp.arange(rounds, dtype=jnp.int32)[None, :, None] * round_span
        + slot_order.reshape(seq_count, 1, 2)
    ).reshape(-1)
    moved = jnp.take(encoded, pick_rows, axis=0).reshape(seq_count, 2 * rounds, encoded.shape[1])
    arrived = lax.all_to_all(moved, "seq", split_axis=0, concat_axis=0, tiled=True)
    all_counts = lax.all_gather(frame_tokens, "seq", axis=0, tiled=True)
    row_block = arrived.reshape(tok_rows, encoded.shape[1])
    columns = row_block
    pre = jnp.dot(
        columns, lax.all_gather(w_in, "seq", axis=0, tiled=True), preferred_element_type=jnp.float32
    )
    hidden_half = jax.nn.gelu(pre + b_in.astype(jnp.float32), approximate=False).astype(
        jnp.bfloat16
    )
    hidden = lax.all_gather(hidden_half, "mp", axis=1, tiled=True)
    columns = hidden
    summed = jnp.dot(
        columns,
        lax.all_gather(w_out, "seq", axis=0, tiled=True),
        preferred_element_type=jnp.float32,
    )
    projected = (summed + b_out.astype(jnp.float32)).astype(jnp.bfloat16)
    owned_slots = lax.dynamic_slice_in_dim(slot_order, own_index * 2, 2)
    local_rows = (
        jnp.arange(rounds, dtype=jnp.int32)[:, None] * round_span + owned_slots[None, :]
    ).reshape(-1)
    frame_ends = jnp.cumsum(all_counts, axis=1)
    finished = frame_ends[:, None, :] <= local_rows[None, :, None]
    frame_local = jnp.sum(finished.astype(jnp.int32), axis=2)
    frame_start = jnp.sum(jnp.where(finished, all_counts[:, None, :], 0), axis=2)
    frame_ids = (
        jnp.arange(seq_count, dtype=jnp.int32)[:, None] * frames_here + frame_local
    ).reshape(-1)
    offsets = (local_rows[None, :] - frame_start).reshape(-1)
    frame_ids, offsets = (frame_ids, offsets)
    wide = projected.astype(jnp.float32)
    square_total = lax.psum(jnp.sum(wide * wide, axis=1), "mp")
    inv_rms = lax.rsqrt(square_total / D + norm_eps)
    half_width = wide.shape[1]
    own_gain = lax.dynamic_slice_in_dim(norm_gain, lax.axis_index("mp") * half_width, half_width)
    normed_half = (wide * inv_rms[:, None] * own_gain.astype(jnp.float32)).astype(jnp.bfloat16)
    normed = lax.all_gather(normed_half, "mp", axis=1, tiled=True)
    columns = normed
    key_linear = jnp.dot(
        columns,
        lax.all_gather(w_key, "seq", axis=0, tiled=True),
        preferred_element_type=jnp.float32,
    )
    value_linear = jnp.dot(
        columns,
        lax.all_gather(w_value, "seq", axis=0, tiled=True),
        preferred_element_type=jnp.float32,
    )
    key_rows = rotate(key_linear + b_key.astype(jnp.float32), frame_ids, offsets).astype(
        jnp.bfloat16
    )
    value_rows = (value_linear + b_value.astype(jnp.float32)).astype(jnp.bfloat16)
    return (key_rows, value_rows)


def solution(mesh):
    return jax.shard_map(
        shards,
        mesh=mesh,
        in_specs=(
            P("seq", None),
            P("seq", None),
            P(),
            P("seq", "mp"),
            P("mp"),
            P("seq", "mp"),
            P("mp"),
            P(),
            P("seq", "mp"),
            P("mp"),
            P("seq", "mp"),
            P("mp"),
        ),
        out_specs=(P("seq", "mp"), P("seq", "mp")),
        check_vma=False,
    )
```

profile of v0, /device:TPU:0, one launch (start us, length us, event | category | flops | bytes accessed | tf_op | source)
XLA Modules:
  0.0 410.8 jit_solution(17500957176617481664)
XLA Ops:
  7.2 0.0 copy-start
  7.2 0.0 all-gather.8.cloned.1.call-start
  7.2 0.7 all-gather.8.cloned.1.call-update
  7.9 2.3 sort.17
  10.2 0.1 add.153
  10.3 0.1 copy.35
  10.3 0.1 broadcast_add_fusion
  10.4 0.1 add.161
  10.6 0.1 add.150
  10.6 0.1 add.151
  10.7 0.1 compare_and_fusion
  10.8 0.1 copy.31
  10.9 0.0 copy-done
  10.9 1.3 gather_fusion
  12.2 0.0 copy-start.2
  12.2 1.0 broadcast_select_fusion
  13.2 8.3 %all-to-all-start = ((bf16[16,16,1152]{2,1,0:T(8,128)(2,1)}), bf16[16,16,1152]{2,1,0:T(8,128)(2,1)S(1)}, u32[]{:S(2)}, u32[]{:S(2)}) async-start(bf16[16,16,1152]{2,1,0:T(8,128)(2,1)} %broadcast_select_fusion), calls=%async_computation | async-start | bytes 1179648 | tf_op jit(solution)/shard_map/all_to_all | solution.py:61
  21.5 0.0 all-gather.10.cloned.1.call-start
  21.6 0.0 copy-done.2
  21.6 21.7 %all-to-all-done = bf16[16,16,1152]{2,1,0:T(8,128)(2,1)S(1)} async-done(((bf16[16,16,1152]{2,1,0:T(8,128)(2,1)}), bf16[16,16,1152]{2,1,0:T(8,128)(2,1)S(1)}, u32[]{:S(2)}, u32[]{:S(2)}) %all-to-all-start) | async-done | bytes 589856 | tf_op jit(solution)/shard_map/all_to_all | solution.py:61
  43.3 50.2 %all-gather.8.cloned.1.call-done = bf16[1152,1792]{1,0:T(8,128)(2,1)} async-done(((bf16[72,1792]{1,0:T(8,128)(2,1)}), bf16[1152,1792]{1,0:T(8,128)(2,1)}) %all-gather.8.cloned.1.call-update) | async-done | bytes 4128784 | tf_op jit(solution)/shard_map/all_gather | solution.py:66
  93.4 7.8 %fusion.4 = bf16[256,1792]{1,0:T(8,128)(2,1)} fusion(bf16[256,1152]{1,0:T(8,128)(2,1)S(1)} %bitcast.18, bf16[1152,1792]{1,0:T(8,128)(2,1)} %all-gather.8.cloned.1.call-done, f32[1792]{0:T(1024)S(1)} %convert_element_type.54), kind=kOutput, calls=%fused_computation.8 | convolution fusion | flops 1087242240 | bytes 5643264 | tf_op jit(solution)/shard_map/dot_general | solution.py:65
  101.3 0.0 copy-start.3
  101.3 0.0 copy-start.4
  101.3 0.0 all-gather.10.cloned.1.call-update
  101.3 0.0 all-gather.12.cloned.1.call-start
  101.4 0.7 all-gather.12.cloned.1.call-update
  102.1 0.0 all-gather.16.cloned.1.call-start
  102.1 0.5 all-gather.16.cloned.1.call-update
  102.6 0.0 all-gather.14.cloned.1.call-start
  102.7 0.0 copy-done.3
  102.7 0.0 copy-done.4
  102.7 0.1 dynamic-slice_convert_fusion
  102.8 7.5 %all-gather.10.cloned.1.call-done = bf16[256,3584]{1,0:T(8,128)(2,1)} async-done(((bf16[256,1792]{1,0:T(8,128)(2,1)}), bf16[256,3584]{1,0:T(8,128)(2,1)}) %all-gather.10.cloned.1.call-update) | async-done | bytes 1835024 | tf_op jit(solution)/shard_map/all_gather | solution.py:71
  110.3 157.8 %all-gather.12.cloned.1.call-done = bf16[3584,1792]{1,0:T(8,128)(2,1)} async-done(((bf16[224,1792]{1,0:T(8,128)(2,1)}), bf16[3584,1792]{1,0:T(8,128)(2,1)}) %all-gather.12.cloned.1.call-update) | async-done | bytes 12845072 | tf_op jit(solution)/shard_map/all_gather | solution.py:75
  268.0 7.7 %multiply_reduce_fusion = (f32[256]{0:T(256)S(1)}, f32[256,1792]{1,0:T(8,128)S(1)}) fusion(f32[1792]{0:T(1024)S(1)} %convert_element_type.56, bf16[256,3584]{1,0:T(8,128)(2,1)} %all-gather.10.cloned.1.call-done, bf16[3584,1792]{1,0:T(8,128)(2,1)} %all-gather.12.cloned.1.call-done), kind=kOutput, calls=%fused_computation.10 | convolution fusion | flops 3290627840 | bytes 16523264 | tf_op jit(solution)/shard_map/dot_general | solution.py:73
  275.7 2.5 psum.7
  278.2 0.0 copy-start.6
  278.2 0.0 copy-start.5
  278.2 0.0 copy-start.7
  278.2 1.2 multiply_convert_fusion
  279.4 0.0 all-gather.14.cloned.1.call-update
  279.4 0.0 all-gather.18.cloned.1.call-start
  279.4 0.5 all-gather.18.cloned.1.call-update
  280.0 0.0 copy-done.6
  280.0 0.1 dynamic_slice.7
  280.1 0.1 add.176
  280.2 0.0 copy-done.5
  280.2 37.8 %all-gather = s32[16,1,2]{2,1,0:T(1,128)S(1)} all-gather(s32[1,1,2]{2,1,0:T(1,128)S(1)} %bitcast.24), channel_id=1, replica_groups=mesh['seq'=16,'mp'=2] {'seq'}, dimensions={0}, use_global_device_ids=true | all-gather | bytes 136 | tf_op jit(solution)/shard_map/all_gather | solution.py:62
  318.0 0.1 copy.32
  318.1 0.1 fusion.15
  318.2 0.1 sub.20
  318.3 0.1 broadcast_add_fusion.1
  318.3 0.1 add.179
  318.4 0.0 copy-done.7
  318.5 0.3 fusion.14
  318.8 9.3 %all-gather.16.cloned.1.call-done = bf16[3584,256]{1,0:T(8,128)(2,1)} async-done(((bf16[224,256]{1,0:T(8,128)(2,1)}), bf16[3584,256]{1,0:T(8,128)(2,1)}) %all-gather.16.cloned.1.call-update) | async-done | bytes 1835024 | tf_op jit(solution)/shard_map/all_gather | solution.py:102
  328.1 10.2 %all-gather.14.cloned.1.call-done = bf16[256,3584]{1,0:T(8,128)(2,1)} async-done(((bf16[256,1792]{1,0:T(8,128)(2,1)}), bf16[256,3584]{1,0:T(8,128)(2,1)}) %all-gather.14.cloned.1.call-update) | async-done | bytes 1835024 | tf_op jit(solution)/shard_map/all_gather | solution.py:98
  338.2 0.0 copy-start.1
  338.2 3.0 convolution_add_fusion.3
  341.4 0.8 copy.34
  342.1 59.1 %all-gather.18.cloned.1.call-done = bf16[3584,256]{1,0:T(8,128)(2,1)} async-done(((bf16[224,256]{1,0:T(8,128)(2,1)}), bf16[3584,256]{1,0:T(8,128)(2,1)}) %all-gather.18.cloned.1.call-update) | async-done | bytes 1835024 | tf_op jit(solution)/shard_map/all_gather | solution.py:107
  401.2 0.0 copy-done.1
  401.2 2.8 fusion.12
  (19 shorter events, 0.2 us)
Async XLA Ops:
  7.2 3.8 copy-start
  7.2 86.3 %all-gather.8.cloned.1.call-start = ((), (), s32[]{:S(2)}) async-start(), calls=%async_computation.1 | async-start | bytes 4386816 | tf_op jit(solution)/shard_map/all_gather | solution.py:66
  12.2 9.4 %copy-start.2 = (bf16[1792]{0:T(1024)(128)(2,1)S(1)}, bf16[1792]{0:T(1024)(128)(2,1)}, u32[]{:S(2)}) copy-start(bf16[1792]{0:T(1024)(128)(2,1)} %param.16) | copy-start | bytes 10756
  13.2 30.1 %all-to-all-start = ((bf16[16,16,1152]{2,1,0:T(8,128)(2,1)}), bf16[16,16,1152]{2,1,0:T(8,128)(2,1)S(1)}, u32[]{:S(2)}, u32[]{:S(2)}) async-start(bf16[16,16,1152]{2,1,0:T(8,128)(2,1)} %broadcast_select_fusion), calls=%async_computation | async-start | bytes 1179648 | tf_op jit(solution)/shard_map/all_to_all | solution.py:61
  21.5 88.7 %all-gather.10.cloned.1.call-start = ((), (), s32[]{:S(2)}) async-start(), calls=%async_computation.2 | async-start | bytes 2752512 | tf_op jit(solution)/shard_map/all_gather | solution.py:71
  101.3 1.4 copy-start.3
  101.3 1.4 copy-start.4
  101.3 166.7 %all-gather.12.cloned.1.call-start = ((), (), s32[]{:S(2)}) async-start(), calls=%async_computation.3 | async-start | bytes 13647872 | tf_op jit(solution)/shard_map/all_gather | solution.py:75
  102.1 226.0 %all-gather.16.cloned.1.call-start = ((), (), s32[]{:S(2)}) async-start(), calls=%async_computation.5 | async-start | bytes 1949696 | tf_op jit(solution)/shard_map/all_gather | solution.py:102
  102.6 235.6 %all-gather.14.cloned.1.call-start = ((), (), s32[]{:S(2)}) async-start(), calls=%async_computation.4 | async-start | bytes 2752512 | tf_op jit(solution)/shard_map/all_gather | solution.py:98
  278.2 1.8 copy-start.6
  278.2 2.0 copy-start.5
  278.2 40.2 %copy-start.7 = (bf16[256]{0:T(256)(128)(2,1)S(1)}, bf16[256]{0:T(256)(128)(2,1)}, u32[]{:S(2)}) copy-start(bf16[256]{0:T(256)(128)(2,1)} %param.23) | copy-start | bytes 1540
  279.4 121.8 %all-gather.18.cloned.1.call-start = ((), (), s32[]{:S(2)}) async-start(), calls=%async_computation.6 | async-start | bytes 1949696 | tf_op jit(solution)/shard_map/all_gather | solution.py:107
  338.2 62.9 %copy-start.1 = (bf16[256,3584]{1,0:T(8,128)(2,1)S(1)}, bf16[256,3584]{1,0:T(8,128)(2,1)}, u32[]{:S(2)}) copy-start(bf16[256,3584]{1,0:T(8,128)(2,1)} %all-gather.14.cloned.1.call-done) | copy-start | bytes 5505028
Sparse Core Ops, SparseCore 0:
  10.8 82.6 all-gather.7
  101.4 8.7 all-gather.9
  113.0 155.0 all-gather.11
  270.6 57.4 all-gather.15
  329.4 8.7 all-gather.13
  340.8 60.3 all-gather.17
where the time goes:
time: 411 us
  waiting for transfers between devices  318 us (77%)
  blocking collectives  40.3 us (10%)
  matrix products  21.4 us (5%)
  between operations  14.3 us (3%)
  starting transfers between devices  8.58 us (2%)
  other arithmetic  5.25 us (1%)
    all_gather x1, waiting for transfers between devices, shards(): lax.all_gather(w_out, 'seq', axis=0, tiled=True)  158 us
    all_gather x1, waiting for transfers between devices, shards(): lax.all_gather(w_value, 'seq', axis=0, tiled=True)  59.1 us
    all_gather x1, waiting for transfers between devices, shards(): lax.all_gather(w_in, 'seq', axis=0, tiled=True)  50.2 us
    all_gather x1, blocking collectives, shards(): all_counts = lax.all_gather(frame_tokens, 'seq', axis=0, tiled=True)  37.8 us
    all_to_all x1, waiting for transfers between devices, shards(): lax.all_to_all(moved, 'seq', split_axis=0, concat_axis=0, tiled=True)  21.7 us
    all_gather x1, waiting for transfers between devices, shards(): normed = lax.all_gather(normed_half, 'mp', axis=1, tiled=True)  10.2 us
    all_gather x1, waiting for transfers between devices, shards(): lax.all_gather(w_key, 'seq', axis=0, tiled=True)  9.27 us
    all_to_all x1, starting transfers between devices, shards(): lax.all_to_all(moved, 'seq', split_axis=0, concat_axis=0, tiled=True)  8.34 us
  transfers between devices with their start and end apart: 7, of which 7 were waited for; matrix products, arithmetic and copies ran while one was open for 5% of the time, Pallas kernels for 0%

commit v1 on v0

--- a/solution.py
+++ b/solution.py
@@ -1,9 +1,10 @@
+import math
+
 import jax
 import jax.numpy as jnp
 from jax import lax
 from jax.sharding import PartitionSpec as P
 
-D = 3584
 HEAD = 128
 TSEC = 16
 
@@ -32,6 +33,29 @@
     return turned.reshape(linear.shape)
 
 
+LANES = 128
+
+
+def fold(block, width):
+    rows, cols = block.shape
+    slots, lanes = width // LANES, cols // LANES
+    pieces = slots // math.gcd(slots, lanes)
+    height = rows // pieces
+    tall = block.reshape(pieces, height, lanes, LANES).transpose(0, 2, 1, 3)
+    tall = tall.reshape(-1, slots, height, LANES).transpose(0, 2, 1, 3)
+    return tall.reshape(-1, width)
+
+
+def unfold(blocks, cols):
+    count, rows, width = blocks.shape
+    slots, lanes = width // LANES, cols // LANES
+    pieces = slots // math.gcd(slots, lanes)
+    height = rows * width // (cols * pieces)
+    tall = blocks.reshape(count, -1, height, slots, LANES).transpose(0, 1, 3, 2, 4)
+    tall = tall.reshape(count, pieces, lanes, height, LANES).transpose(0, 1, 3, 2, 4)
+    return tall.reshape(-1, cols)
+
+
 def shards(
     encoded,
     frame_tokens,
@@ -47,6 +71,15 @@
     b_value,
 ):
     seq_count = lax.axis_size("seq")
+    in_rows, out_rows = w_in.shape[0], w_out.shape[0]
+    kv_width = w_key.shape[1] + w_value.shape[1]
+    packed = jnp.concatenate(
+        [w_in, w_out, fold(jnp.concatenate([w_key, w_value], axis=1), w_in.shape[1])], axis=0
+    )
+    whole = lax.all_gather(packed, "seq", axis=0)
+    all_in = whole[:, :in_rows].reshape(-1, w_in.shape[1])
+    all_out = whole[:, in_rows : in_rows + out_rows].reshape(-1, w_out.shape[1])
+    all_kv = unfold(whole[:, in_rows + out_rows :], kv_width)
     own_index = lax.axis_index("seq")
     tok_rows = encoded.shape[0]
     round_span = 2 * seq_count
@@ -63,7 +96,7 @@
     row_block = arrived.reshape(tok_rows, encoded.shape[1])
     columns = row_block
     pre = jnp.dot(
-        columns, lax.all_gather(w_in, "seq", axis=0, tiled=True), preferred_element_type=jnp.float32
+        columns, all_in, preferred_element_type=jnp.float32
     )
     hidden_half = jax.nn.gelu(pre + b_in.astype(jnp.float32), approximate=False).astype(
         jnp.bfloat16
@@ -72,7 +105,7 @@
     columns = hidden
     summed = jnp.dot(
         columns,
-        lax.all_gather(w_out, "seq", axis=0, tiled=True),
+        all_out,
         preferred_element_type=jnp.float32,
     )
     projected = (summed + b_out.astype(jnp.float32)).astype(jnp.bfloat16)
@@ -89,24 +122,12 @@
     ).reshape(-1)
     offsets = (local_rows[None, :] - frame_start).reshape(-1)
     frame_ids, offsets = (frame_ids, offsets)
-    wide = projected.astype(jnp.float32)
-    square_total = lax.psum(jnp.sum(wide * wide, axis=1), "mp")
-    inv_rms = lax.rsqrt(square_total / D + norm_eps)
-    half_width = wide.shape[1]
-    own_gain = lax.dynamic_slice_in_dim(norm_gain, lax.axis_index("mp") * half_width, half_width)
-    normed_half = (wide * inv_rms[:, None] * own_gain.astype(jnp.float32)).astype(jnp.bfloat16)
-    normed = lax.all_gather(normed_half, "mp", axis=1, tiled=True)
-    columns = normed
-    key_linear = jnp.dot(
-        columns,
-        lax.all_gather(w_key, "seq", axis=0, tiled=True),
-        preferred_element_type=jnp.float32,
-    )
-    value_linear = jnp.dot(
-        columns,
-        lax.all_gather(w_value, "seq", axis=0, tiled=True),
-        preferred_element_type=jnp.float32,
-    )
+    wide = lax.all_gather(projected, "mp", axis=1, tiled=True).astype(jnp.float32)
+    inv_rms = lax.rsqrt(jnp.mean(wide * wide, axis=1) + norm_eps)
+    normed = (wide * inv_rms[:, None] * norm_gain.astype(jnp.float32)).astype(jnp.bfloat16)
+    both = jnp.dot(normed, all_kv, preferred_element_type=jnp.float32)
+    key_linear = both[:, : w_key.shape[1]]
+    value_linear = both[:, w_key.shape[1] :]
     key_rows = rotate(key_linear + b_key.astype(jnp.float32), frame_ids, offsets).astype(
         jnp.bfloat16
     )

time: 411 us -> 361 us (0.88)
  waiting for transfers between devices: 318 us -> 230 us
  local copies, waits for them, and re-layouts: 3.03 us -> 40.1 us
  other arithmetic: 5.25 us -> 9.41 us
    all_gather x5 -> x2, waiting for transfers between devices: 286 us -> 230 us  [the longest x1 230 us: shards(): whole = lax.all_gather(packed, 'seq', axis=0)]
    all_to_all x1, waiting for transfers between devices: 21.7 us -> 0.01 us  [shards(): lax.all_to_all(moved, 'seq', split_axis=0, concat_axis=0, tiled=True)]
    slice x0 -> x3, local copies, waits for them, and re-layouts: none -> 20.8 us  [the longest x1 12.2 us: shards(): all_out = whole[:, in_rows:in_rows + out_rows].reshape(-1, w_out.shape[1])]
    transpose x0 -> x4, local copies, waits for them, and re-layouts: none -> 8.73 us  [the longest x1 5.47 us: unfold(): tall.reshape(count, pieces, lanes, height, LANES).transpose(0, 1, 3, 2, 4)]
    reshape x0 -> x3, local copies, waits for them, and re-layouts: none -> 7.57 us  [the longest x1 7.38 us: unfold(): blocks.reshape(count, -1, height, slots, LANES).transpose(0, 1, 3, 2, 4)]
    all_gather x1, waiting for transfers between devices: 7.46 us -> 0.01 us  [shards(): hidden = lax.all_gather(hidden_half, 'mp', axis=1, tiled=True)]
    dot_general x4 -> x3, matrix products: 21.4 us -> 20.7 us  [the longest x1 9.65 us: shards(): summed = jnp.dot(columns, all_out, preferred_element_type=jnp.float32)]
  transfers between devices with their start and end apart: 7 -> 4, of which waited for: 7 -> 1; matrix products, arithmetic and copies ran while one was open for 5% -> 12% of each run, Pallas kernels for 0% -> 0%
where the time goes in v1:
time: 361 us
  waiting for transfers between devices  230 us (64%)
  local copies, waits for them, and re-layouts  40.1 us (11%)
  blocking collectives  38 us (11%)
  matrix products  20.7 us (6%)
  between operations  14 us (4%)
  other arithmetic  9.41 us (3%)
  starting transfers between devices  8.46 us (2%)
    all_gather x1, waiting for transfers between devices, shards(): whole = lax.all_gather(packed, 'seq', axis=0)  230 us
    all_gather x1, blocking collectives, shards(): all_counts = lax.all_gather(frame_tokens, 'seq', axis=0, tiled=True)  38 us
    slice x1, local copies, waits for them, and re-layouts, shards(): all_out = whole[:, in_rows:in_rows + out_rows].reshape(-1, w_out.shape[1])  12.2 us
    dot_general x1, matrix products, shards(): summed = jnp.dot(columns, all_out, preferred_element_type=jnp.float32)  9.65 us
    all_to_all x1, starting transfers between devices, shards(): lax.all_to_all(moved, 'seq', split_axis=0, concat_axis=0, tiled=True)  8.34 us
    dot_general x1, matrix products, shards(): pre = jnp.dot(columns, all_in, preferred_element_type=jnp.float32)  7.79 us
    reshape x1, local copies, waits for them, and re-layouts, unfold(): blocks.reshape(count, -1, height, slots, LANES).transpose(0, 1, 3, 2, 4)  7.38 us
  transfers between devices with their start and end apart: 4, of which 1 were waited for; matrix products, arithmetic and copies ran while one was open for 12% of the time, Pallas kernels for 0%

profile of v1, /device:TPU:0, one launch (start us, length us, event | category | flops | bytes accessed | tf_op | source)
XLA Modules:
  0.0 360.7 jit_solution(2350747890977966903)
XLA Ops:
  7.2 0.0 copy-start
  7.2 0.0 copy-start.3
  7.2 0.0 copy-start.2
  7.2 0.0 all-gather.10.cloned.1.call-start
  7.2 1.1 pad_maximum_fusion.1
  8.3 0.1 reshape.270
  8.4 0.1 copy.46
  8.5 0.1 copy.60
  8.6 0.0 copy-done.3
  8.6 0.0 copy-done.2
  8.6 0.0 copy-start.8
  8.6 1.2 pad_maximum_fusion
  9.8 0.0 all-gather.10.cloned.1.call-update
  9.8 0.1 add.149
  9.9 0.1 add.150
  10.0 0.0 copy-done.8
  10.0 1.6 sort.17
  11.6 0.1 add.152
  11.7 0.1 copy.50
  11.8 0.1 compare_and_fusion
  11.8 0.1 copy.44
  11.9 0.1 broadcast_add_fusion
  12.0 0.1 add.160
  12.2 0.0 copy-done
  12.2 1.3 gather_fusion
  13.5 0.0 copy-start.5
  13.5 1.0 broadcast_select_fusion
  14.5 8.3 %all-to-all-start = ((bf16[16,16,1152]{2,1,0:T(8,128)(2,1)}), bf16[16,16,1152]{2,1,0:T(8,128)(2,1)S(1)}, u32[]{:S(2)}, u32[]{:S(2)}) async-start(bf16[16,16,1152]{2,1,0:T(8,128)(2,1)} %broadcast_select_fusion), calls=%async_computation | async-start | bytes 1179648 | tf_op jit(solution)/shard_map/all_to_all | solution.py:94
  22.8 0.0 all-gather.6.cloned.1.call-start
  22.9 0.0 copy-done.5
  22.9 229.9 %all-gather.10.cloned.1.call-done = bf16[5760,1792]{1,0:T(8,128)(2,1)} async-done(((bf16[360,1792]{1,0:T(8,128)(2,1)}), bf16[5760,1792]{1,0:T(8,128)(2,1)}) %all-gather.10.cloned.1.call-update) | async-done | bytes 20643856 | tf_op jit(solution)/shard_map/all_gather | solution.py:79
  252.8 4.4 %slice.30 = bf16[16,72,1792]{2,1,0:T(8,128)(2,1)} slice(bf16[16,360,1792]{2,1,0:T(8,128)(2,1)} %bitcast.35), slice={[0:16], [0:72], [0:1792]} | slice | bytes 8257536 | tf_op jit(solution)/shard_map/slice | solution.py:80
  257.2 0.0 all-to-all-done
  257.2 7.8 %fusion.9 = bf16[256,1792]{1,0:T(8,128)(2,1)} fusion(bf16[256,1152]{1,0:T(8,128)(2,1)S(1)} %bitcast.48, bf16[1152,1792]{1,0:T(8,128)(2,1)} %bitcast.41, f32[1792]{0:T(1024)S(1)} %convert_element_type.54), kind=kOutput, calls=%fused_computation.15 | convolution fusion | flops 1087242240 | bytes 5643264 | tf_op jit(solution)/shard_map/dot_general | solution.py:98
  265.0 0.0 all-gather.6.cloned.1.call-update
  265.0 0.0 all-gather.8.cloned.1.call-start
  265.1 0.0 copy-done.6
  265.1 12.2 %slice.31 = bf16[16,224,1792]{2,1,0:T(8,128)(2,1)} slice(bf16[16,360,1792]{2,1,0:T(8,128)(2,1)} %bitcast.36), slice={[0:16], [72:296], [0:1792]} | slice | bytes 25690112 | tf_op jit(solution)/shard_map/slice | solution.py:81
  277.3 0.0 copy-start.10
  277.3 9.7 %fusion.6 = bf16[256,1792]{1,0:T(8,128)(2,1)} fusion(bf16[256,3584]{1,0:T(8,128)(2,1)} %all-gather.6.cloned.1.call-done, bf16[3584,1792]{1,0:T(8,128)(2,1)} %bitcast.40, f32[1792]{0:T(1024)S(1)} %convert_element_type.56), kind=kOutput, calls=%fused_computation.12 | convolution fusion | flops 3289251840 | bytes 15604736 | tf_op jit(solution)/shard_map/dot_general | solution.py:106
  287.0 0.0 all-gather.8.cloned.1.call-update
  287.0 0.1 dynamic_slice.3
  287.1 0.1 add.174
  287.2 0.0 copy-done.7
  287.2 38.0 %all-gather.1 = s32[16,1,2]{2,1,0:T(1,128)S(1)} all-gather(s32[1,1,2]{2,1,0:T(1,128)S(1)} %bitcast.55), channel_id=1, replica_groups=mesh['seq'=16,'mp'=2] {'seq'}, dimensions={0}, use_global_device_ids=true | all-gather | bytes 136 | tf_op jit(solution)/shard_map/all_gather | solution.py:95
  325.2 0.1 copy.49
  325.3 0.1 fusion.23
  325.4 0.1 sub.20
  325.4 0.1 broadcast_add_fusion.1
  325.5 0.1 add.177
  325.6 0.0 copy-done.4
  325.7 0.5 fusion.22
  326.2 4.2 %slice.32 = bf16[16,64,1792]{2,1,0:T(8,128)(2,1)} slice(bf16[16,360,1792]{2,1,0:T(8,128)(2,1)} %bitcast.37), slice={[0:16], [296:360], [0:1792]} | slice | bytes 7340032 | tf_op jit(solution)/shard_map/slice | solution.py:82
  330.5 7.4 %reshape.275 = bf16[16,2,32,14,128]{4,3,2,1,0:T(8,128)(2,1)} reshape(bf16[16,64,1792]{2,1,0:T(8,128)(2,1)} %slice.32) | data formatting | bytes 7340032 | tf_op jit(solution)/shard_map/reshape | solution.py:54
  337.9 3.1 copy.47
  341.0 5.5 %copy.48 = bf16[16,7,32,4,128]{4,3,2,1,0:T(4,128)(2,1)} copy(bf16[16,7,32,4,128]{4,2,3,1,0:T(8,128)(2,1)S(1)} %bitcast.39) | data formatting | bytes 7340032 | tf_op jit(solution)/shard_map/transpose | solution.py:55
  346.5 2.1 fusion
  348.6 0.0 copy-done.1
  348.6 3.2 fusion.3
  351.8 0.7 fusion.20
  352.5 0.1 reshape.278
  352.6 0.5 subtract_convert_fusion
  353.1 0.4 pad_maximum_fusion.2
  353.5 0.7 copy.61
  (28 shorter events, 0.2 us)
Async XLA Ops:
  7.2 5.0 %copy-start = (bf16[256,1152]{1,0:T(8,128)(2,1)S(1)}, bf16[256,1152]{1,0:T(8,128)(2,1)}, u32[]{:S(2)}) copy-start(bf16[256,1152]{1,0:T(8,128)(2,1)} %param.12) | copy-start | bytes 1769476
  7.2 1.4 copy-start.3
  7.2 1.4 copy-start.2
  7.2 245.6 %all-gather.10.cloned.1.call-start = ((), (), s32[]{:S(2)}) async-start(), calls=%async_computation.3 | async-start | bytes 21934080 | tf_op jit(solution)/shard_map/all_gather | solution.py:79
  8.6 1.4 copy-start.8
  13.5 9.4 %copy-start.5 = (bf16[1792]{0:T(1024)(128)(2,1)S(1)}, bf16[1792]{0:T(1024)(128)(2,1)}, u32[]{:S(2)}) copy-start(bf16[1792]{0:T(1024)(128)(2,1)} %param.16) | copy-start | bytes 10756
  14.5 242.7 %all-to-all-start = ((bf16[16,16,1152]{2,1,0:T(8,128)(2,1)}), bf16[16,16,1152]{2,1,0:T(8,128)(2,1)S(1)}, u32[]{:S(2)}, u32[]{:S(2)}) async-start(bf16[16,16,1152]{2,1,0:T(8,128)(2,1)} %broadcast_select_fusion), calls=%async_computation | async-start | bytes 1179648 | tf_op jit(solution)/shard_map/all_to_all | solution.py:94
  22.8 254.5 %all-gather.6.cloned.1.call-start = ((), (), s32[]{:S(2)}) async-start(), calls=%async_computation.1 | async-start | bytes 2752512 | tf_op jit(solution)/shard_map/all_gather | solution.py:104
  257.2 7.9 %copy-start.6 = (bf16[1792]{0:T(1024)(128)(2,1)S(1)}, bf16[1792]{0:T(1024)(128)(2,1)}, u32[]{:S(2)}) copy-start(bf16[1792]{0:T(1024)(128)(2,1)} %param.18) | copy-start | bytes 10756
  265.0 81.4 %all-gather.8.cloned.1.call-start = ((), (), s32[]{:S(2)}) async-start(), calls=%async_computation.2 | async-start | bytes 2752512 | tf_op jit(solution)/shard_map/all_gather | solution.py:125
  277.3 9.9 %copy-start.7 = (s32[1,2]{1,0:T(1,128)S(1)}, s32[1,2]{1,0:T(1,128)}, u32[]{:S(2)}) copy-start(s32[1,2]{1,0:T(1,128)} %param.13) | copy-start | bytes 28
  277.3 48.3 %copy-start.4 = (bf16[3584]{0:T(1024)(128)(2,1)S(1)}, bf16[3584]{0:T(1024)(128)(2,1)}, u32[]{:S(2)}) copy-start(bf16[3584]{0:T(1024)(128)(2,1)} %param.19) | copy-start | bytes 21508
  277.3 48.3 %copy-start.9 = (bf16[256]{0:T(256)(128)(2,1)S(1)}, bf16[256]{0:T(256)(128)(2,1)}, u32[]{:S(2)}) copy-start(bf16[256]{0:T(256)(128)(2,1)} %param.21) | copy-start | bytes 1540
  277.3 48.3 %copy-start.10 = (bf16[256]{0:T(256)(128)(2,1)S(1)}, bf16[256]{0:T(256)(128)(2,1)}, u32[]{:S(2)}) copy-start(bf16[256]{0:T(256)(128)(2,1)} %param.23) | copy-start | bytes 1540
  346.5 2.1 copy-start.1
Sparse Core Ops, SparseCore 0:
  10.8 241.9 all-gather.9
  265.1 8.3 all-gather.5
  287.1 8.3 all-gather.7

commit v2 on v0

v2 whole, which is shorter than its diff:
```python
import jax
import jax.numpy as jnp
from jax import lax
from jax.sharding import PartitionSpec as P

HEAD = 128
TSEC = 16


norm_eps = 1e-06
rope_base = 1000000.0


def rotate(linear, frame_ids, offsets):
    pairs = HEAD // 2
    pair_index = jnp.arange(pairs)
    inverse = jnp.power(jnp.float32(rope_base), -2.0 * pair_index.astype(jnp.float32) / HEAD)
    chosen = jnp.where(pair_index[None, :] < TSEC, frame_ids[:, None], offsets[:, None]).astype(
        jnp.float32
    )
    angles = chosen * inverse[None, :]
    cosine = jnp.cos(angles)[:, None, :]
    sine = jnp.sin(angles)[:, None, :]
    shaped = linear.reshape(linear.shape[0], -1, HEAD)
    first_half = shaped[..., :pairs]
    second_half = shaped[..., pairs:]
    turned = jnp.concatenate(
        [first_half * cosine - second_half * sine, second_half * cosine + first_half * sine],
        axis=-1,
    )
    return turned.reshape(linear.shape)


PAIR = 2


def both(block, axis):
    other = lax.ppermute(block, axis, [(0, 1), (1, 0)])
    first = lax.axis_index(axis) == 0
    return jnp.where(first, block, other), jnp.where(first, other, block)


def swapped(zeroth, oneth, axis):
    first = lax.axis_index(axis) == 0
    kept = jnp.where(first, zeroth, oneth)
    other = lax.ppermute(jnp.where(first, oneth, zeroth), axis, [(0, 1), (1, 0)])
    return jnp.where(first, kept, other), jnp.where(first, other, kept)


def shards(
    encoded,
    frame_tokens,
    slot_owner,
    w_in,
    b_in,
    w_out,
    b_out,
    norm_gain,
    w_key,
    b_key,
    w_value,
    b_value,
):
    seq = ("o", "i")
    seq_count = lax.axis_size("o") * lax.axis_size("i")
    own_index = lax.axis_index(seq)
    pair_index = lax.axis_index("i")
    tok_rows = encoded.shape[0]
    quarter = w_in.shape[1] // PAIR
    round_span = 2 * seq_count
    rounds = tok_rows // round_span
    frames_here = frame_tokens.shape[1]

    in_rows = jnp.concatenate(swapped(w_in[:, :quarter], w_in[:, quarter:], "i"), axis=0)
    all_in = lax.all_gather(in_rows, "o", axis=0, tiled=True)
    out_rows = jnp.concatenate(swapped(w_out[:, :quarter], w_out[:, quarter:], "i"), axis=0)
    kv_rows = jnp.concatenate(both(jnp.concatenate([w_key, w_value], axis=1), "i"), axis=0)
    late = lax.all_gather(jnp.concatenate([out_rows, kv_rows], axis=1), "o", axis=0, tiled=True)

    slot_order = jnp.argsort(slot_owner, stable=True)
    pick_rows = (
        jnp.arange(rounds, dtype=jnp.int32)[None, :, None] * round_span
        + slot_order.reshape(seq_count, 1, 2)
    ).reshape(-1)
    moved = jnp.take(encoded, pick_rows, axis=0).reshape(seq_count, 2 * rounds, encoded.shape[1])
    arrived = lax.all_to_all(moved, seq, split_axis=0, concat_axis=0, tiled=True)
    all_counts = lax.all_gather(frame_tokens, seq, axis=0, tiled=True)
    arrived, all_counts = lax.optimization_barrier((arrived, all_counts))
    row_block = arrived.reshape(tok_rows, encoded.shape[1])
    columns = jnp.concatenate(both(row_block, "i"), axis=0)
    own_b_in = lax.dynamic_slice_in_dim(b_in, pair_index * quarter, quarter)
    own_b_out = lax.dynamic_slice_in_dim(b_out, pair_index * quarter, quarter)
    pre = jnp.dot(columns, all_in, preferred_element_type=jnp.float32)
    hidden = jax.nn.gelu(pre + own_b_in.astype(jnp.float32), approximate=False).astype(
        jnp.bfloat16
    )
    hidden = jnp.concatenate(both(hidden, "i"), axis=1)
    hidden = jnp.concatenate(both(hidden, "mp"), axis=1)
    summed = jnp.dot(hidden, late[:, :quarter], preferred_element_type=jnp.float32)
    projected = (summed + own_b_out.astype(jnp.float32)).astype(jnp.bfloat16)
    projected = jnp.concatenate(
        swapped(projected[:tok_rows], projected[tok_rows:], "i"), axis=1
    )
    wide = jnp.concatenate(both(projected, "mp"), axis=1).astype(jnp.float32)

    owned_slots = lax.dynamic_slice_in_dim(slot_order, own_index * 2, 2)
    local_rows = (
        jnp.arange(rounds, dtype=jnp.int32)[:, None] * round_span + owned_slots[None, :]
    ).reshape(-1)
    frame_ends = jnp.cumsum(all_counts, axis=1)
    finished = frame_ends[:, None, :] <= local_rows[None, :, None]
    frame_local = jnp.sum(finished.astype(jnp.int32), axis=2)
    frame_start = jnp.sum(jnp.where(finished, all_counts[:, None, :], 0), axis=2)
    frame_ids = (
        jnp.arange(seq_count, dtype=jnp.int32)[:, None] * frames_here + frame_local
    ).reshape(-1)
    offsets = (local_rows[None, :] - frame_start).reshape(-1)

    inv_rms = lax.rsqrt(jnp.mean(wide * wide, axis=1) + norm_eps)
    normed = (wide * inv_rms[:, None] * norm_gain.astype(jnp.float32)).astype(jnp.bfloat16)
    linear = jnp.dot(normed, late[:, quarter:], preferred_element_type=jnp.float32)
    key_linear = linear[:, : w_key.shape[1]]
    value_linear = linear[:, w_key.shape[1] :]
    key_rows = rotate(key_linear + b_key.astype(jnp.float32), frame_ids, offsets).astype(
        jnp.bfloat16
    )
    value_rows = (value_linear + b_value.astype(jnp.float32)).astype(jnp.bfloat16)
    return (key_rows, value_rows)


def solution(mesh):
    seq_count, mp_count = mesh.shape["seq"], mesh.shape["mp"]
    paired = jax.sharding.Mesh(
        mesh.devices.reshape(seq_count // PAIR, PAIR, mp_count), ("o", "i", "mp")
    )
    seq = ("o", "i")
    return jax.shard_map(
        shards,
        mesh=paired,
        in_specs=(
            P(seq, None),
            P(seq, None),
            P(),
            P(seq, "mp"),
            P("mp"),
            P(seq, "mp"),
            P("mp"),
            P(),
            P(seq, "mp"),
            P("mp"),
            P(seq, "mp"),
            P("mp"),
        ),
        out_specs=(P(seq, "mp"), P(seq, "mp")),
        check_vma=False,
    )
```

time: 411 us -> 259 us (0.63)
  waiting for transfers between devices: 318 us -> 137 us
  blocking collectives: 40.3 us -> 52.6 us
  other arithmetic: 5.25 us -> 17.1 us
  starting transfers between devices: 8.58 us -> 16.5 us
    all_gather x6 -> x2, waiting for transfers between devices: 294 us -> 81.7 us  [the longest x1 81.7 us: shards(): lax.all_gather(jnp.concatenate([out_rows, kv_rows], axis=1), 'o', axis=0,...]
    ppermute x0 -> x8, waiting for transfers between devices: none -> 54.9 us  [the longest x5 34.5 us: both(): other = lax.ppermute(block, axis, [(0, 1), (1, 0)])]
    all_to_all x1, waiting for transfers between devices: 21.7 us -> 0.01 us  [shards(): lax.all_to_all(moved, seq, split_axis=0, concat_axis=0, tiled=True)]
    all_gather x1, blocking collectives: 37.8 us -> 52.6 us  [shards(): all_counts = lax.all_gather(frame_tokens, seq, axis=0, tiled=True)]
    ppermute x0 -> x8, starting transfers between devices: none -> 9.58 us  [the longest x3 4.92 us: swapped(): lax.ppermute(jnp.where(first, oneth, zeroth), axis, [(0, 1), (1, 0)])]
    select_n x0 -> x11, other arithmetic: none -> 7.31 us  [the longest x5 4.9 us: both(): return (jnp.where(first, block, other), jnp.where(first, other, block))]
    dot_general x4 -> x3, matrix products: 21.4 us -> 18.5 us  [the longest x1 7.9 us: shards(): jnp.dot(hidden, late[:, :quarter], preferred_element_type=jnp.float32)]
  transfers between devices with their start and end apart: 7 -> 11, of which waited for: 7 -> 9; matrix products, arithmetic and copies ran while one was open for 5% -> 8% of each run, Pallas kernels for 0% -> 0%
where the time goes in v2:
time: 259 us
  waiting for transfers between devices  137 us (53%)
  blocking collectives  52.6 us (20%)
  matrix products  18.5 us (7%)
  other arithmetic  17.1 us (7%)
  starting transfers between devices  16.5 us (6%)
  between operations  14.4 us (6%)
  local copies, waits for them, and re-layouts  3.14 us (1%)
    all_gather x1, waiting for transfers between devices, shards(): lax.all_gather(jnp.concatenate([out_rows, kv_rows], axis=1), 'o', axis=0,...  81.7 us
    all_gather x1, blocking collectives, shards(): all_counts = lax.all_gather(frame_tokens, seq, axis=0, tiled=True)  52.6 us
    ppermute x5, waiting for transfers between devices, both(): other = lax.ppermute(block, axis, [(0, 1), (1, 0)])  34.5 us
    ppermute x3, waiting for transfers between devices, swapped(): lax.ppermute(jnp.where(first, oneth, zeroth), axis, [(0, 1), (1, 0)])  20.4 us
    dot_general x1, matrix products, shards(): jnp.dot(hidden, late[:, :quarter], preferred_element_type=jnp.float32)  7.9 us
    dot_general x1, matrix products, shards(): pre = jnp.dot(columns, all_in, preferred_element_type=jnp.float32)  7.31 us
    all_to_all x1, starting transfers between devices, shards(): lax.all_to_all(moved, seq, split_axis=0, concat_axis=0, tiled=True)  6.83 us
  transfers between devices with their start and end apart: 11, of which 9 were waited for; matrix products, arithmetic and copies ran while one was open for 8% of the time, Pallas kernels for 0%

profile of v2, /device:TPU:0, one launch (start us, length us, event | category | flops | bytes accessed | tf_op | source)
XLA Modules:
  0.0 258.8 jit_solution(740917860373496108)
XLA Ops:
  7.2 0.0 all-gather.4.cloned.1.call-start
  7.3 1.1 broadcast_select_fusion.21
  8.4 3.0 %collective-permute-start.1 = (bf16[72,896]{1,0:T(8,128)(2,1)S(1)}, bf16[72,896]{1,0:T(8,128)(2,1)S(1)}, u32[]{:S(2)}, u32[]{:S(2)}) collective-permute-start(bf16[72,896]{1,0:T(8,128)(2,1)S(1)} %broadcast_select_fusion.21), channel_id=1, source_target_pairs={{0,2},{2,0},{1,3},{3,1},{4,6},{6,4},{5,7},{7,5},{8,10},{10,8},{9,1... | collective-permute-start | bytes 387080 | tf_op jit(solution)/shard_map/ppermute | solution.py:46
  11.4 3.5 %collective-permute-done.1 = bf16[72,896]{1,0:T(8,128)(2,1)S(1)} collective-permute-done((bf16[72,896]{1,0:T(8,128)(2,1)S(1)}, bf16[72,896]{1,0:T(8,128)(2,1)S(1)}, u32[]{:S(2)}, u32[]{:S(2)}) %collective-permute-start.1) | collective-permute-done | bytes 129056 | tf_op jit(solution)/shard_map/ppermute | solution.py:46
  14.8 1.0 broadcast_select_fusion.20
  15.8 0.7 pad_maximum_fusion.4
  16.6 0.0 all-gather.6.cloned.1.call-start
  16.7 1.8 collective-permute-start.5
  18.5 0.1 broadcast_select_fusion.15
  18.6 0.4 collective-permute-start.4
  18.9 6.3 %collective-permute-done.5 = bf16[224,512]{1,0:T(8,128)(2,1)S(1)} collective-permute-done((bf16[224,512]{1,0:T(8,128)(2,1)S(1)}, bf16[224,512]{1,0:T(8,128)(2,1)S(1)}, u32[]{:S(2)}, u32[]{:S(2)}) %collective-permute-start.5) | collective-permute-done | bytes 229408 | tf_op jit(solution)/shard_map/ppermute | solution.py:38
  25.3 6.9 %collective-permute-done.4 = bf16[224,896]{1,0:T(8,128)(2,1)S(1)} collective-permute-done((bf16[224,896]{1,0:T(8,128)(2,1)S(1)}, bf16[224,896]{1,0:T(8,128)(2,1)S(1)}, u32[]{:S(2)}, u32[]{:S(2)}) %collective-permute-start.4) | collective-permute-done | bytes 401440 | tf_op jit(solution)/shard_map/ppermute | solution.py:46
  32.2 0.1 broadcast_select_fusion.14
  32.3 1.1 maximum_maximum_fusion
  33.5 1.6 sort.17
  35.1 0.1 add.159
  35.1 0.1 copy.30
  35.2 0.1 add.156
  35.3 0.1 add.157
  35.4 0.1 compare_and_fusion
  35.5 0.1 copy.28
  35.6 0.1 broadcast_add_fusion
  35.6 0.1 add.167
  35.8 1.3 gather_fusion
  37.1 1.0 broadcast_select_fusion.6
  38.1 6.8 %all-to-all-start = ((bf16[16,16,1152]{2,1,0:T(8,128)(2,1)}), bf16[16,16,1152]{2,1,0:T(8,128)(2,1)S(1)}, u32[]{:S(2)}, u32[]{:S(2)}) async-start(bf16[16,16,1152]{2,1,0:T(8,128)(2,1)} %broadcast_select_fusion.6), calls=%async_computation | async-start | bytes 1179648 | tf_op jit(solution)/shard_map/all_to_all | solution.py:86
  45.0 52.6 %all-gather = s32[16,1,2]{2,1,0:T(1,128)S(1)} all-gather(s32[1,1,2]{2,1,0:T(1,128)S(1)} %bitcast.21), channel_id=1, replica_groups=mesh['o'=8,'i'=2,'mp'=2] {'o','i'}, dimensions={0}, use_global_device_ids=true | all-gather | bytes 136 | tf_op jit(solution)/shard_map/all_gather | solution.py:87
  97.6 0.1 copy.29
  97.6 1.5 collective-permute-start
  99.1 0.1 dynamic-slice_convert_fusion.1
  99.2 11.4 %collective-permute-done = bf16[256,1152]{1,0:T(8,128)(2,1)S(1)} collective-permute-done((bf16[256,1152]{1,0:T(8,128)(2,1)S(1)}, bf16[256,1152]{1,0:T(8,128)(2,1)S(1)}, u32[]{:S(2)}, u32[]{:S(2)}) %collective-permute-start) | collective-permute-done | bytes 589856 | tf_op jit(solution)/shard_map/ppermute | solution.py:38
  110.6 0.2 broadcast_select_fusion.8
  110.8 7.3 %fusion.12 = bf16[512,896]{1,0:T(8,128)(2,1)S(1)} fusion(bf16[1152,896]{1,0:T(8,128)(2,1)} %all-gather.4.cloned.1.call-done, bf16[256,1152]{1,0:T(8,128)(2,1)S(1)} %get-tuple-element.21, bf16[256,1152]{1,0:T(8,128)(2,1)S(1)} %get-tuple-element.20, f32[896]{0:T(1024)S(1)} %dynamic-slice_convert_fusion.1), kind=kOutput, calls=%fused_computation.16 | convolution fusion | flops 1089601536 | bytes 4165120 | tf_op jit(solution)/shard_map/dot_general | solution.py:93
  118.1 1.3 collective-permute-start.2
  119.4 12.1 %collective-permute-done.2 = bf16[512,896]{1,0:T(8,128)(2,1)S(1)} collective-permute-done((bf16[512,896]{1,0:T(8,128)(2,1)S(1)}, bf16[512,896]{1,0:T(8,128)(2,1)S(1)}, u32[]{:S(2)}, u32[]{:S(2)}) %collective-permute-start.2) | collective-permute-done | bytes 917536 | tf_op jit(solution)/shard_map/ppermute | solution.py:38
  131.6 0.2 broadcast_select_fusion.3
  131.8 1.4 pad_maximum_fusion
  133.2 0.1 dynamic-slice_convert_fusion
  133.3 4.0 %collective-permute-done.3 = bf16[512,1792]{1,0:T(8,128)(2,1)} collective-permute-done((bf16[512,1792]{1,0:T(8,128)(2,1)}, bf16[512,1792]{1,0:T(8,128)(2,1)}, u32[]{:S(2)}, u32[]{:S(2)}) %collective-permute-start.3) | collective-permute-done | bytes 1835040 | tf_op jit(solution)/shard_map/ppermute | solution.py:38
  137.3 4.2 %broadcast_select_fusion.1 = (bf16[512,1792]{1,0:T(8,128)(2,1)}, bf16[512,1792]{1,0:T(8,128)(2,1)}) fusion(bf16[512,1792]{1,0:T(8,128)(2,1)} %collective-permute-done.3, pred[]{:T(512)S(6)} %eq.4, bf16[512,896]{1,0:T(8,128)(2,1)S(1)} %get-tuple-element.15, bf16[512,896]{1,0:T(8,128)(2,1)S(1)} %get-tuple-element.14), kind=kLoop, calls=%fused_computation.38 | loop fusion | flops 5505024 | bytes 7340033 | tf_op jit(solution)/shard_map/jit(_where)/select_n | solution.py:40
  141.5 81.7 %all-gather.6.cloned.1.call-done = bf16[3584,1408]{1,0:T(8,128)(2,1)} async-done(((bf16[448,1408]{1,0:T(8,128)(2,1)}), bf16[3584,1408]{1,0:T(8,128)(2,1)}) %all-gather.6.cloned.1.call-update) | async-done | bytes 10092560 | tf_op jit(solution)/shard_map/all_gather | solution.py:78
  223.2 7.9 %add_convert_fusion = bf16[512,896]{1,0:T(8,128)(2,1)S(1)} fusion(bf16[3584,1408]{1,0:T(8,128)(2,1)} %all-gather.6.cloned.1.call-done, bf16[512,1792]{1,0:T(8,128)(2,1)} %get-tuple-element.11, bf16[512,1792]{1,0:T(8,128)(2,1)} %get-tuple-element.10, f32[896]{0:T(1024)S(1)} %dynamic-slice_convert_fusion), kind=kOutput, calls=%fused_computation.21 | convolution fusion | flops 3296591872 | bytes 11013632 | tf_op jit(solution)/shard_map/dot_general | solution.py:99
  231.1 0.1 broadcast_select_fusion.11
  231.2 1.5 collective-permute-start.6
  232.7 10.1 %collective-permute-done.6 = bf16[256,896]{1,0:T(8,128)(2,1)S(1)} collective-permute-done((bf16[256,896]{1,0:T(8,128)(2,1)S(1)}, bf16[256,896]{1,0:T(8,128)(2,1)S(1)}, u32[]{:S(2)}, u32[]{:S(2)}) %collective-permute-start.6) | collective-permute-done | bytes 458784 | tf_op jit(solution)/shard_map/ppermute | solution.py:46
  242.8 0.1 broadcast_select_fusion.10
  242.9 0.1 pad_maximum_fusion.3
  243.0 0.1 collective-permute-start.7
  243.1 0.1 dynamic_slice.11
  243.2 0.1 add.183
  243.4 0.1 fusion.33
  243.5 0.1 broadcast_subtract_fusion
  243.5 0.1 add.186
  243.6 0.1 sub.20
  243.7 1.2 fusion.32
  244.9 0.6 collective-permute-done.7
  245.5 0.3 broadcast_select_fusion.5
  245.9 0.4 fusion.2
  246.3 3.3 %fusion.5 = f32[256,512]{1,0:T(8,128)S(1)} fusion(bf16[3584,1408]{1,0:T(8,128)(2,1)} %all-gather.6.cloned.1.call-done, f32[3584]{0:T(1024)S(1)} %convert_element_type.59, f32[256]{0:T(256)S(1)} %add_rsqrt_fusion, bf16[256,1792]{1,0:T(8,128)(2,1)S(1)} %get-tuple-element.13, bf16[256,1792]{1,0:T(8,128)(2,1)S(1)} %get-tuple-element.12), kind=kOutput, calls=%fused_computation.8 | convolution fusion | flops 945946624 | bytes 6044672 | tf_op jit(solution)/shard_map/dot_general | solution.py:121
  249.6 0.7 fusion.30
  250.3 0.1 reshape.246
  250.5 0.5 subtract_convert_fusion
  251.0 0.4 pad_maximum_fusion.5
  251.3 0.7 copy.33
  (47 shorter events, 0.3 us)
Async XLA Ops:
  7.2 28.6 %copy-start = (bf16[256,1152]{1,0:T(8,128)(2,1)S(1)}, bf16[256,1152]{1,0:T(8,128)(2,1)}, u32[]{:S(2)}) copy-start(bf16[256,1152]{1,0:T(8,128)(2,1)} %param.12) | copy-start | bytes 1769476
  7.2 9.5 %copy-start.3 = (bf16[224,256]{1,0:T(8,128)(2,1)S(1)}, bf16[224,256]{1,0:T(8,128)(2,1)}, u32[]{:S(2)}) copy-start(bf16[224,256]{1,0:T(8,128)(2,1)} %param.20) | copy-start | bytes 344068
  7.2 9.5 %copy-start.4 = (bf16[224,256]{1,0:T(8,128)(2,1)S(1)}, bf16[224,256]{1,0:T(8,128)(2,1)}, u32[]{:S(2)}) copy-start(bf16[224,256]{1,0:T(8,128)(2,1)} %param.22) | copy-start | bytes 344068
  7.2 11.3 %copy-start.1 = (bf16[224,1792]{1,0:T(8,128)(2,1)S(1)}, bf16[224,1792]{1,0:T(8,128)(2,1)}, u32[]{:S(2)}) copy-start(bf16[224,1792]{1,0:T(8,128)(2,1)} %param.17) | copy-start | bytes 2408452
  7.2 103.6 %all-gather.4.cloned.1.call-start = ((), (), s32[]{:S(2)}) async-start(), calls=%async_computation.1 | async-start | bytes 2322432 | tf_op jit(solution)/shard_map/all_gather | solution.py:75
  8.4 6.5 %collective-permute-start.1 = (bf16[72,896]{1,0:T(8,128)(2,1)S(1)}, bf16[72,896]{1,0:T(8,128)(2,1)S(1)}, u32[]{:S(2)}, u32[]{:S(2)}) collective-permute-start(bf16[72,896]{1,0:T(8,128)(2,1)S(1)} %broadcast_select_fusion.21), channel_id=1, source_target_pairs={{0,2},{2,0},{1,3},{3,1},{4,6},{6,4},{5,7},{7,5},{8,10},{10,8},{9,1... | collective-permute-start | bytes 387080 | tf_op jit(solution)/shard_map/ppermute | solution.py:46
  16.6 206.6 %all-gather.6.cloned.1.call-start = ((), (), s32[]{:S(2)}) async-start(), calls=%async_computation.2 | async-start | bytes 11354112 | tf_op jit(solution)/shard_map/all_gather | solution.py:78
  16.7 8.5 %collective-permute-start.5 = (bf16[224,512]{1,0:T(8,128)(2,1)S(1)}, bf16[224,512]{1,0:T(8,128)(2,1)S(1)}, u32[]{:S(2)}, u32[]{:S(2)}) collective-permute-start(bf16[224,512]{1,0:T(8,128)(2,1)S(1)} %constant_dynamic-update-slice_fusion), channel_id=1, source_target_pairs={{0,2},{2,0},{1,3},{3,1},{4,6},{6,4},{5,7},{7,5},{8,10},{10,8},{9,1... | collective-permute-start | bytes 688136 | tf_op jit(solution)/shard_map/ppermute | solution.py:38
  18.6 13.6 %collective-permute-start.4 = (bf16[224,896]{1,0:T(8,128)(2,1)S(1)}, bf16[224,896]{1,0:T(8,128)(2,1)S(1)}, u32[]{:S(2)}, u32[]{:S(2)}) collective-permute-start(bf16[224,896]{1,0:T(8,128)(2,1)S(1)} %broadcast_select_fusion.15), channel_id=1, source_target_pairs={{0,2},{2,0},{1,3},{3,1},{4,6},{6,4},{5,7},{7,5},{8,10},{10,8},{9,1... | collective-permute-start | bytes 1204232 | tf_op jit(solution)/shard_map/ppermute | solution.py:46
  32.2 1.2 copy-start.9
  37.1 7.9 %copy-start.8 = (s32[1,2]{1,0:T(1,128)S(1)}, s32[1,2]{1,0:T(1,128)}, u32[]{:S(2)}) copy-start(s32[1,2]{1,0:T(1,128)} %param.13) | copy-start | bytes 28
  37.1 62.0 %copy-start.6 = (bf16[1792]{0:T(1024)(128)(2,1)S(1)}, bf16[1792]{0:T(1024)(128)(2,1)}, u32[]{:S(2)}) copy-start(bf16[1792]{0:T(1024)(128)(2,1)} %param.16) | copy-start | bytes 10756
  38.1 59.5 %all-to-all-start = ((bf16[16,16,1152]{2,1,0:T(8,128)(2,1)}), bf16[16,16,1152]{2,1,0:T(8,128)(2,1)S(1)}, u32[]{:S(2)}, u32[]{:S(2)}) async-start(bf16[16,16,1152]{2,1,0:T(8,128)(2,1)} %broadcast_select_fusion.6), calls=%async_computation | async-start | bytes 1179648 | tf_op jit(solution)/shard_map/all_to_all | solution.py:86
  97.6 12.9 %collective-permute-start = (bf16[256,1152]{1,0:T(8,128)(2,1)S(1)}, bf16[256,1152]{1,0:T(8,128)(2,1)S(1)}, u32[]{:S(2)}, u32[]{:S(2)}) collective-permute-start(bf16[256,1152]{1,0:T(8,128)(2,1)S(1)} %bitcast.13), channel_id=1, source_target_pairs={{0,2},{2,0},{1,3},{3,1},{4,6},{6,4},{5,7},{7,5},{8,10},{10,8},{9,1... | collective-permute-start | bytes 1769480 | tf_op jit(solution)/shard_map/ppermute | solution.py:38
  118.1 13.5 %collective-permute-start.2 = (bf16[512,896]{1,0:T(8,128)(2,1)S(1)}, bf16[512,896]{1,0:T(8,128)(2,1)S(1)}, u32[]{:S(2)}, u32[]{:S(2)}) collective-permute-start(bf16[512,896]{1,0:T(8,128)(2,1)S(1)} %fusion.12), channel_id=1, source_target_pairs={{0,2},{2,0},{1,3},{3,1},{4,6},{6,4},{5,7},{7,5},{8,10},{10,8},{9,1... | collective-permute-start | bytes 2752520 | tf_op jit(solution)/shard_map/ppermute | solution.py:38
  131.7 1.5 copy-start.7
  133.2 4.1 %collective-permute-start.3 = (bf16[512,1792]{1,0:T(8,128)(2,1)}, bf16[512,1792]{1,0:T(8,128)(2,1)}, u32[]{:S(2)}, u32[]{:S(2)}) collective-permute-start(bf16[512,1792]{1,0:T(8,128)(2,1)} %pad_maximum_fusion), channel_id=1, source_target_pairs={{0,1},{1,0},{2,3},{3,2},{4,5},{5,4},{6,7},{7,6},{8,9},{9,8},{10,11... | collective-permute-start | bytes 5505032 | tf_op jit(solution)/shard_map/ppermute | solution.py:38
  231.1 11.9 %copy-start.5 = (bf16[3584]{0:T(1024)(128)(2,1)S(1)}, bf16[3584]{0:T(1024)(128)(2,1)}, u32[]{:S(2)}) copy-start(bf16[3584]{0:T(1024)(128)(2,1)} %param.19) | copy-start | bytes 21508
  231.2 11.9 %copy-start.10 = (bf16[256]{0:T(256)(128)(2,1)S(1)}, bf16[256]{0:T(256)(128)(2,1)}, u32[]{:S(2)}) copy-start(bf16[256]{0:T(256)(128)(2,1)} %param.21) | copy-start | bytes 1540
  231.2 11.9 %copy-start.11 = (bf16[256]{0:T(256)(128)(2,1)S(1)}, bf16[256]{0:T(256)(128)(2,1)}, u32[]{:S(2)}) copy-start(bf16[256]{0:T(256)(128)(2,1)} %param.23) | copy-start | bytes 1540
  231.2 11.6 %collective-permute-start.6 = (bf16[256,896]{1,0:T(8,128)(2,1)S(1)}, bf16[256,896]{1,0:T(8,128)(2,1)S(1)}, u32[]{:S(2)}, u32[]{:S(2)}) collective-permute-start(bf16[256,896]{1,0:T(8,128)(2,1)S(1)} %broadcast_select_fusion.11), channel_id=1, source_target_pairs={{0,2},{2,0},{1,3},{3,1},{4,6},{6,4},{5,7},{7,5},{8,10},{10,8},{9,1... | collective-permute-start | bytes 1376264 | tf_op jit(solution)/shard_map/ppermute | solution.py:46
  243.0 2.5 collective-permute-start.7
  246.3 4.1 %copy-start.2 = (f32[256,64]{1,0:T(8,128)S(1)}, f32[256,64]{1,0:T(8,128)}, u32[]{:S(2)}) copy-start(f32[256,64]{1,0:T(8,128)} %get-tuple-element.31) | copy-start | bytes 196612
Sparse Core Ops, SparseCore 0:
  16.7 59.4 all-gather.3
  78.4 144.7 all-gather.5

commit v3 on v2

--- a/solution.py
+++ b/solution.py
@@ -32,6 +32,7 @@
 
 
 PAIR = 2
+LANES = 128
 
 
 def both(block, axis):
@@ -71,8 +72,6 @@
     rounds = tok_rows // round_span
     frames_here = frame_tokens.shape[1]
 
-    in_rows = jnp.concatenate(swapped(w_in[:, :quarter], w_in[:, quarter:], "i"), axis=0)
-    all_in = lax.all_gather(in_rows, "o", axis=0, tiled=True)
     out_rows = jnp.concatenate(swapped(w_out[:, :quarter], w_out[:, quarter:], "i"), axis=0)
     kv_rows = jnp.concatenate(both(jnp.concatenate([w_key, w_value], axis=1), "i"), axis=0)
     late = lax.all_gather(jnp.concatenate([out_rows, kv_rows], axis=1), "o", axis=0, tiled=True)
@@ -83,24 +82,41 @@
         + slot_order.reshape(seq_count, 1, 2)
     ).reshape(-1)
     moved = jnp.take(encoded, pick_rows, axis=0).reshape(seq_count, 2 * rounds, encoded.shape[1])
+    counts = jnp.pad(frame_tokens[0].astype(jnp.bfloat16), (0, LANES - frames_here))
+    counts = jnp.broadcast_to(counts, moved.shape[:2] + (LANES,))
+    moved = jnp.concatenate([moved, counts], axis=2)
     arrived = lax.all_to_all(moved, seq, split_axis=0, concat_axis=0, tiled=True)
-    all_counts = lax.all_gather(frame_tokens, seq, axis=0, tiled=True)
-    arrived, all_counts = lax.optimization_barrier((arrived, all_counts))
-    row_block = arrived.reshape(tok_rows, encoded.shape[1])
-    columns = jnp.concatenate(both(row_block, "i"), axis=0)
+    all_counts = arrived[:, 0, encoded.shape[1] :][:, :frames_here].astype(jnp.int32)
+    row_block = arrived[:, :, : encoded.shape[1]].reshape(tok_rows, encoded.shape[1])
+    parts = jnp.stack([w_in[:, :quarter], w_in[:, quarter:]])
+    parts = jnp.broadcast_to(parts[None], (lax.axis_size("o"),) + parts.shape)
+    all_in = lax.all_to_all(
+        parts.reshape(seq_count, -1, quarter), seq, split_axis=0, concat_axis=0, tiled=True
+    ).reshape(-1, quarter)
+    swap = [(0, 1), (1, 0)]
+    first = pair_index == 0
+    columns = jnp.concatenate([lax.ppermute(row_block, "i", swap), row_block], axis=0)
     own_b_in = lax.dynamic_slice_in_dim(b_in, pair_index * quarter, quarter)
     own_b_out = lax.dynamic_slice_in_dim(b_out, pair_index * quarter, quarter)
     pre = jnp.dot(columns, all_in, preferred_element_type=jnp.float32)
     hidden = jax.nn.gelu(pre + own_b_in.astype(jnp.float32), approximate=False).astype(
         jnp.bfloat16
     )
-    hidden = jnp.concatenate(both(hidden, "i"), axis=1)
+    other = lax.ppermute(hidden, "i", swap)
+    other = jnp.concatenate([other[tok_rows:], other[:tok_rows]], axis=0)
+    hidden = jnp.concatenate(
+        [jnp.where(first, hidden, other), jnp.where(first, other, hidden)], axis=1
+    )
     hidden = jnp.concatenate(both(hidden, "mp"), axis=1)
-    summed = jnp.dot(hidden, late[:, :quarter], preferred_element_type=jnp.float32)
-    projected = (summed + own_b_out.astype(jnp.float32)).astype(jnp.bfloat16)
-    projected = jnp.concatenate(
-        swapped(projected[:tok_rows], projected[tok_rows:], "i"), axis=1
-    )
+
+    def project(rows):
+        summed = jnp.dot(rows, late[:, :quarter], preferred_element_type=jnp.float32)
+        return (summed + own_b_out.astype(jnp.float32)).astype(jnp.bfloat16)
+
+    got = lax.ppermute(project(hidden[:tok_rows]), "i", swap)
+    kept = project(hidden[tok_rows:])
+    got, kept = lax.optimization_barrier((got, kept))
+    projected = jnp.concatenate([jnp.where(first, kept, got), jnp.where(first, got, kept)], axis=1)
     wide = jnp.concatenate(both(projected, "mp"), axis=1).astype(jnp.float32)
 
     owned_slots = lax.dynamic_slice_in_dim(slot_order, own_index * 2, 2)

time: 259 us -> 258 us (level)
  blocking collectives: 52.6 us -> 0 us
  waiting for transfers between devices: 137 us -> 175 us
  starting transfers between devices: 16.5 us -> 27.5 us
  local copies, waits for them, and re-layouts: 3.14 us -> 6.85 us
    all_gather x1 -> x0, blocking collectives: 52.6 us -> none  [shards(): all_counts = lax.all_gather(frame_tokens, seq, axis=0, tiled=True)]
    ppermute x0 -> x3, waiting for transfers between devices: none -> 45.1 us  [the longest x1 20.8 us: shards(): other = lax.ppermute(hidden, 'i', swap)]
    all_to_all x0 -> x1, waiting for transfers between devices: none -> 35.6 us  [shards(): lax.all_to_all(parts.reshape(seq_count, -1, quarter), seq, split_axis=0,...]
    all_gather x1, waiting for transfers between devices: 81.7 us -> 48.7 us  [shards(): lax.all_gather(jnp.concatenate([out_rows, kv_rows], axis=1), 'o', axis=0,...]
    all_to_all x1, waiting for transfers between devices: 0.01 us -> 27.6 us  [shards(): lax.all_to_all(moved, seq, split_axis=0, concat_axis=0, tiled=True)]
    ppermute x5 -> x3, waiting for transfers between devices: 34.5 us -> 10.3 us  [both(): other = lax.ppermute(block, axis, [(0, 1), (1, 0)])]
    all_to_all x0 -> x1, starting transfers between devices: none -> 12.8 us  [shards(): lax.all_to_all(parts.reshape(seq_count, -1, quarter), seq, split_axis=0,...]
    ppermute x3 -> x1, waiting for transfers between devices: 20.4 us -> 7.71 us  [swapped(): lax.ppermute(jnp.where(first, oneth, zeroth), axis, [(0, 1), (1, 0)])]
  transfers between devices with their start and end apart: 11 -> 10, of which waited for: 9 -> 10; matrix products, arithmetic and copies ran while one was open for 8% -> 9% of each run, Pallas kernels for 0% -> 0%
where the time goes in v3:
time: 258 us
  waiting for transfers between devices  175 us (68%)
  starting transfers between devices  27.5 us (11%)
  matrix products  18.1 us (7%)
  other arithmetic  15.9 us (6%)
  between operations  14.4 us (6%)
  local copies, waits for them, and re-layouts  6.85 us (3%)
    all_gather x1, waiting for transfers between devices, shards(): lax.all_gather(jnp.concatenate([out_rows, kv_rows], axis=1), 'o', axis=0,...  48.7 us
    all_to_all x1, waiting for transfers between devices, shards(): lax.all_to_all(parts.reshape(seq_count, -1, quarter), seq, split_axis=0,...  35.6 us
    all_to_all x1, waiting for transfers between devices, shards(): lax.all_to_all(moved, seq, split_axis=0, concat_axis=0, tiled=True)  27.6 us
    ppermute x1, waiting for transfers between devices, shards(): other = lax.ppermute(hidden, 'i', swap)  20.8 us
    ppermute x1, waiting for transfers between devices, shards(): lax.ppermute(row_block, 'i', swap)  15.7 us
    all_to_all x1, starting transfers between devices, shards(): lax.all_to_all(parts.reshape(seq_count, -1, quarter), seq, split_axis=0,...  12.8 us
    ppermute x3, waiting for transfers between devices, both(): other = lax.ppermute(block, axis, [(0, 1), (1, 0)])  10.3 us
    ppermute x1, waiting for transfers between devices, shards(): got = lax.ppermute(project(hidden[:tok_rows]), 'i', swap)  8.58 us
  transfers between devices with their start and end apart: 10, of which 10 were waited for; matrix products, arithmetic and copies ran while one was open for 9% of the time, Pallas kernels for 0%

profile of v3, /device:TPU:0, one launch (start us, length us, event | category | flops | bytes accessed | tf_op | source)
XLA Modules:
  0.0 258.0 jit_solution(10555977737998645100)
XLA Ops:
  7.2 1.0 constant_dynamic-update-slice_fusion.1
  8.2 0.9 constant_dynamic-update-slice_fusion
  9.1 3.0 %collective-permute-start.4 = (bf16[224,512]{1,0:T(8,128)(2,1)S(1)}, bf16[224,512]{1,0:T(8,128)(2,1)S(1)}, u32[]{:S(2)}, u32[]{:S(2)}) collective-permute-start(bf16[224,512]{1,0:T(8,128)(2,1)S(1)} %constant_dynamic-update-slice_fusion), channel_id=1, source_target_pairs={{0,2},{2,0},{1,3},{3,1},{4,6},{6,4},{5,7},{7,5},{8,10},{10,8},{9,1... | collective-permute-start | bytes 688136 | tf_op jit(solution)/shard_map/ppermute | solution.py:39
  12.1 1.2 broadcast_select_fusion.11
  13.3 0.1 collective-permute-start.3
  13.4 5.2 %collective-permute-done.4 = bf16[224,512]{1,0:T(8,128)(2,1)S(1)} collective-permute-done((bf16[224,512]{1,0:T(8,128)(2,1)S(1)}, bf16[224,512]{1,0:T(8,128)(2,1)S(1)}, u32[]{:S(2)}, u32[]{:S(2)}) %collective-permute-start.4) | collective-permute-done | bytes 229408 | tf_op jit(solution)/shard_map/ppermute | solution.py:39
  18.6 7.7 %collective-permute-done.3 = bf16[224,896]{1,0:T(8,128)(2,1)S(1)} collective-permute-done((bf16[224,896]{1,0:T(8,128)(2,1)S(1)}, bf16[224,896]{1,0:T(8,128)(2,1)S(1)}, u32[]{:S(2)}, u32[]{:S(2)}) %collective-permute-start.3) | collective-permute-done | bytes 401440 | tf_op jit(solution)/shard_map/ppermute | solution.py:47
  26.3 0.1 broadcast_select_fusion.10
  26.4 1.1 maximum_maximum_fusion
  27.6 1.6 sort.17
  29.2 0.1 add.167
  29.3 0.1 copy.23
  29.4 0.1 add.164
  29.5 0.1 add.165
  29.6 0.1 compare_and_fusion
  29.6 0.1 copy.19
  29.7 0.1 broadcast_add_fusion
  29.8 0.1 add.175
  30.0 1.3 gather_fusion
  31.3 0.1 broadcast_select_fusion.6
  31.5 1.0 pad_maximum_fusion.11
  32.4 7.1 %all-to-all-start = ((bf16[16,16,1280]{2,1,0:T(8,128)(2,1)}), bf16[16,16,1280]{2,1,0:T(8,128)(2,1)S(1)}, u32[]{:S(2)}, u32[]{:S(2)}) async-start(bf16[16,16,1280]{2,1,0:T(8,128)(2,1)} %pad_maximum_fusion.11), calls=%async_computation | async-start | bytes 1310720 | tf_op jit(solution)/shard_map/all_to_all | solution.py:88
  39.6 27.6 %all-to-all-done = bf16[16,16,1280]{2,1,0:T(8,128)(2,1)S(1)} async-done(((bf16[16,16,1280]{2,1,0:T(8,128)(2,1)}), bf16[16,16,1280]{2,1,0:T(8,128)(2,1)S(1)}, u32[]{:S(2)}, u32[]{:S(2)}) %all-to-all-start) | async-done | bytes 655392 | tf_op jit(solution)/shard_map/all_to_all | solution.py:88
  67.3 1.5 broadcast_in_dim.53
  68.8 12.8 %all-to-all-start.1 = ((bf16[16,72,896]{2,1,0:T(8,128)(2,1)}), bf16[16,72,896]{2,1,0:T(8,128)(2,1)}, u32[]{:S(2)}, u32[]{:S(2)}) async-start(bf16[16,72,896]{2,1,0:T(8,128)(2,1)} %bitcast.7), calls=%async_computation.1 | async-start | bytes 4128768 | tf_op jit(solution)/shard_map/all_to_all | solution.py:93
  81.6 1.9 collective-permute-start
  83.6 0.1 dynamic-slice_convert_fusion.1
  83.6 15.7 %collective-permute-done = bf16[256,1152]{1,0:T(8,128)(2,1)S(1)} collective-permute-done((bf16[256,1152]{1,0:T(8,128)(2,1)S(1)}, bf16[256,1152]{1,0:T(8,128)(2,1)S(1)}, u32[]{:S(2)}, u32[]{:S(2)}) %collective-permute-start) | collective-permute-done | bytes 589856 | tf_op jit(solution)/shard_map/ppermute | solution.py:98
  99.3 35.6 %all-to-all-done.1 = bf16[16,72,896]{2,1,0:T(8,128)(2,1)} async-done(((bf16[16,72,896]{2,1,0:T(8,128)(2,1)}), bf16[16,72,896]{2,1,0:T(8,128)(2,1)}, u32[]{:S(2)}, u32[]{:S(2)}) %all-to-all-start.1) | async-done | bytes 2064416 | tf_op jit(solution)/shard_map/all_to_all | solution.py:93
  135.0 7.3 %fusion.11 = bf16[512,896]{1,0:T(8,128)(2,1)S(1)} fusion(bf16[1152,896]{1,0:T(8,128)(2,1)} %bitcast.8, bf16[256,1152]{1,0:T(8,128)(2,1)S(1)} %bitcast.22, bf16[256,1152]{1,0:T(8,128)(2,1)S(1)} %collective-permute-done, f32[896]{0:T(1024)S(1)} %dynamic-slice_convert_fusion.1), kind=kOutput, calls=%fused_computation.17 | convolution fusion | flops 1089601536 | bytes 4165120 | tf_op jit(solution)/shard_map/dot_general | solution.py:101
  142.2 0.9 collective-permute-start.1
  143.1 20.8 %collective-permute-done.1 = bf16[512,896]{1,0:T(8,128)(2,1)S(1)} collective-permute-done((bf16[512,896]{1,0:T(8,128)(2,1)S(1)}, bf16[512,896]{1,0:T(8,128)(2,1)S(1)}, u32[]{:S(2)}, u32[]{:S(2)}) %collective-permute-start.1) | collective-permute-done | bytes 917536 | tf_op jit(solution)/shard_map/ppermute | solution.py:105
  163.9 0.1 fusion.54
  164.0 0.4 broadcast_select_fusion.3
  164.4 1.4 pad_maximum_fusion.2
  165.8 0.1 dynamic-slice_convert_fusion
  165.9 4.0 %collective-permute-done.2 = bf16[512,1792]{1,0:T(8,128)(2,1)} collective-permute-done((bf16[512,1792]{1,0:T(8,128)(2,1)}, bf16[512,1792]{1,0:T(8,128)(2,1)}, u32[]{:S(2)}, u32[]{:S(2)}) %collective-permute-start.2) | collective-permute-done | bytes 1835040 | tf_op jit(solution)/shard_map/ppermute | solution.py:39
  169.9 4.0 %broadcast_select_fusion = (bf16[512,1792]{1,0:T(8,128)(2,1)}, bf16[512,1792]{1,0:T(8,128)(2,1)}) fusion(bf16[512,1792]{1,0:T(8,128)(2,1)} %collective-permute-done.2, pred[]{:T(512)S(6)} %eq.4, bf16[512,896]{1,0:T(8,128)(2,1)S(1)} %get-tuple-element.15, bf16[512,896]{1,0:T(8,128)(2,1)S(1)} %get-tuple-element.14), kind=kLoop, calls=%fused_computation.40 | loop fusion | flops 5505024 | bytes 7340033 | tf_op jit(solution)/shard_map/jit(_where)/select_n | solution.py:41
  173.9 48.7 %all-gather.2.cloned.1.call-done = bf16[3584,1408]{1,0:T(8,128)(2,1)} async-done(((bf16[448,1408]{1,0:T(8,128)(2,1)}), bf16[3584,1408]{1,0:T(8,128)(2,1)}) %all-gather.2.cloned.1.call-update) | async-done | bytes 10092560 | tf_op jit(solution)/shard_map/all_gather | solution.py:77
  222.7 5.6 %fusion.36 = bf16[256,896]{1,0:T(8,128)(2,1)S(1)} fusion(bf16[3584,1408]{1,0:T(8,128)(2,1)} %all-gather.2.cloned.1.call-done, bf16[512,1792]{1,0:T(8,128)(2,1)} %get-tuple-element.11, bf16[512,1792]{1,0:T(8,128)(2,1)} %get-tuple-element.10, f32[896]{0:T(1024)S(1)} %dynamic-slice_convert_fusion), kind=kOutput, calls=%fused_computation.45 | convolution fusion | flops 1648295936 | bytes 10554880 | tf_op jit(solution)/shard_map/dot_general | solution.py:113
  228.3 1.7 collective-permute-start.5
  229.9 0.1 copy-done.8
  230.0 2.1 fusion.33
  232.1 8.6 %collective-permute-done.5 = bf16[256,896]{1,0:T(8,128)(2,1)S(1)} collective-permute-done((bf16[256,896]{1,0:T(8,128)(2,1)S(1)}, bf16[256,896]{1,0:T(8,128)(2,1)S(1)}, u32[]{:S(2)}, u32[]{:S(2)}) %collective-permute-start.5) | collective-permute-done | bytes 458784 | tf_op jit(solution)/shard_map/ppermute | solution.py:116
  240.7 0.1 broadcast_select_fusion.8
  241.1 0.1 dynamic_slice.11
  241.1 0.1 add.192
  241.3 0.2 reduce_window_sum.11
  241.4 0.1 copy.21
  241.5 0.1 copy.20
  241.6 0.1 fusion.47
  241.7 0.1 broadcast_subtract_fusion
  241.7 0.1 add.195
  241.8 0.1 sub.20
  241.9 0.6 fusion.46
  242.5 1.1 collective-permute-done.6
  243.6 1.5 broadcast_select_fusion.5
  245.1 0.4 fusion.4
  245.5 3.2 %fusion.7 = f32[256,512]{1,0:T(8,128)S(1)} fusion(bf16[3584,1408]{1,0:T(8,128)(2,1)} %all-gather.2.cloned.1.call-done, f32[3584]{0:T(1024)S(1)} %convert_element_type.77, f32[256]{0:T(256)S(1)} %add_rsqrt_fusion, bf16[256,1792]{1,0:T(8,128)(2,1)S(1)} %get-tuple-element.13, bf16[256,1792]{1,0:T(8,128)(2,1)S(1)} %get-tuple-element.12), kind=kOutput, calls=%fused_computation.10 | convolution fusion | flops 945946624 | bytes 6044672 | tf_op jit(solution)/shard_map/dot_general | solution.py:137
  248.7 0.7 fusion.44
  249.4 0.1 reshape.256
  249.6 0.5 subtract_convert_fusion
  250.1 0.4 pad_maximum_fusion.13
  250.5 0.7 copy.27
  (53 shorter events, 0.5 us)
Async XLA Ops:
  7.2 22.8 %copy-start = (bf16[256,1152]{1,0:T(8,128)(2,1)S(1)}, bf16[256,1152]{1,0:T(8,128)(2,1)}, u32[]{:S(2)}) copy-start(bf16[256,1152]{1,0:T(8,128)(2,1)} %param.12) | copy-start | bytes 1769476
  7.2 19.1 %copy-start.1 = (bf16[224,1792]{1,0:T(8,128)(2,1)S(1)}, bf16[224,1792]{1,0:T(8,128)(2,1)}, u32[]{:S(2)}) copy-start(bf16[224,1792]{1,0:T(8,128)(2,1)} %param.17) | copy-start | bytes 2408452
  7.2 215.5 %all-gather.2.cloned.1.call-start = ((), (), s32[]{:S(2)}) async-start(), calls=%async_computation.2 | async-start | bytes 11354112 | tf_op jit(solution)/shard_map/all_gather | solution.py:77
  9.1 9.4 %collective-permute-start.4 = (bf16[224,512]{1,0:T(8,128)(2,1)S(1)}, bf16[224,512]{1,0:T(8,128)(2,1)S(1)}, u32[]{:S(2)}, u32[]{:S(2)}) collective-permute-start(bf16[224,512]{1,0:T(8,128)(2,1)S(1)} %constant_dynamic-update-slice_fusion), channel_id=1, source_target_pairs={{0,2},{2,0},{1,3},{3,1},{4,6},{6,4},{5,7},{7,5},{8,10},{10,8},{9,1... | collective-permute-start | bytes 688136 | tf_op jit(solution)/shard_map/ppermute | solution.py:39
  13.3 13.0 %collective-permute-start.3 = (bf16[224,896]{1,0:T(8,128)(2,1)S(1)}, bf16[224,896]{1,0:T(8,128)(2,1)S(1)}, u32[]{:S(2)}, u32[]{:S(2)}) collective-permute-start(bf16[224,896]{1,0:T(8,128)(2,1)S(1)} %broadcast_select_fusion.11), channel_id=1, source_target_pairs={{0,2},{2,0},{1,3},{3,1},{4,6},{6,4},{5,7},{7,5},{8,10},{10,8},{9,1... | collective-permute-start | bytes 1204232 | tf_op jit(solution)/shard_map/ppermute | solution.py:47
  26.4 1.2 copy-start.9
  30.0 1.3 copy-start.10
  31.3 8.2 %copy-start.4 = (bf16[72,1792]{1,0:T(8,128)(2,1)S(1)}, bf16[72,1792]{1,0:T(8,128)(2,1)}, u32[]{:S(2)}) copy-start(bf16[72,1792]{1,0:T(8,128)(2,1)} %param.15) | copy-start | bytes 774148
  32.4 34.8 %all-to-all-start = ((bf16[16,16,1280]{2,1,0:T(8,128)(2,1)}), bf16[16,16,1280]{2,1,0:T(8,128)(2,1)S(1)}, u32[]{:S(2)}, u32[]{:S(2)}) async-start(bf16[16,16,1280]{2,1,0:T(8,128)(2,1)} %pad_maximum_fusion.11), calls=%async_computation | async-start | bytes 1310720 | tf_op jit(solution)/shard_map/all_to_all | solution.py:88
  68.8 14.8 %copy-start.6 = (bf16[1792]{0:T(1024)(128)(2,1)S(1)}, bf16[1792]{0:T(1024)(128)(2,1)}, u32[]{:S(2)}) copy-start(bf16[1792]{0:T(1024)(128)(2,1)} %param.16) | copy-start | bytes 10756
  68.8 66.2 %all-to-all-start.1 = ((bf16[16,72,896]{2,1,0:T(8,128)(2,1)}), bf16[16,72,896]{2,1,0:T(8,128)(2,1)}, u32[]{:S(2)}, u32[]{:S(2)}) async-start(bf16[16,72,896]{2,1,0:T(8,128)(2,1)} %bitcast.7), calls=%async_computation.1 | async-start | bytes 4128768 | tf_op jit(solution)/shard_map/all_to_all | solution.py:93
  81.6 17.7 %collective-permute-start = (bf16[256,1152]{1,0:T(8,128)(2,1)S(1)}, bf16[256,1152]{1,0:T(8,128)(2,1)S(1)}, u32[]{:S(2)}, u32[]{:S(2)}) collective-permute-start(bf16[256,1152]{1,0:T(8,128)(2,1)S(1)} %bitcast.21), channel_id=1, source_target_pairs={{0,2},{2,0},{1,3},{3,1},{4,6},{6,4},{5,7},{7,5},{8,10},{10,8},{9,1... | collective-permute-start | bytes 1769480 | tf_op jit(solution)/shard_map/ppermute | solution.py:98
  142.2 21.7 %collective-permute-start.1 = (bf16[512,896]{1,0:T(8,128)(2,1)S(1)}, bf16[512,896]{1,0:T(8,128)(2,1)S(1)}, u32[]{:S(2)}, u32[]{:S(2)}) collective-permute-start(bf16[512,896]{1,0:T(8,128)(2,1)S(1)} %fusion.11), channel_id=1, source_target_pairs={{0,2},{2,0},{1,3},{3,1},{4,6},{6,4},{5,7},{7,5},{8,10},{10,8},{9,1... | collective-permute-start | bytes 2752520 | tf_op jit(solution)/shard_map/ppermute | solution.py:105
  164.3 1.5 copy-start.7
  165.8 4.1 %collective-permute-start.2 = (bf16[512,1792]{1,0:T(8,128)(2,1)}, bf16[512,1792]{1,0:T(8,128)(2,1)}, u32[]{:S(2)}, u32[]{:S(2)}) collective-permute-start(bf16[512,1792]{1,0:T(8,128)(2,1)} %pad_maximum_fusion.2), channel_id=1, source_target_pairs={{0,1},{1,0},{2,3},{3,2},{4,5},{5,4},{6,7},{7,6},{8,9},{9,8},{10,11... | collective-permute-start | bytes 5505032 | tf_op jit(solution)/shard_map/ppermute | solution.py:39
  222.7 7.3 %copy-start.2 = (bf16[512,1792]{1,0:T(8,128)(2,1)S(1)}, bf16[512,1792]{1,0:T(8,128)(2,1)}, u32[]{:S(2)}) copy-start(bf16[512,1792]{1,0:T(8,128)(2,1)} %get-tuple-element.10) | copy-start | bytes 5505028
  222.7 7.3 %copy-start.3 = (bf16[512,1792]{1,0:T(8,128)(2,1)S(1)}, bf16[512,1792]{1,0:T(8,128)(2,1)}, u32[]{:S(2)}) copy-start(bf16[512,1792]{1,0:T(8,128)(2,1)} %get-tuple-element.11) | copy-start | bytes 5505028
  222.7 7.4 %copy-start.8 = (bf16[3584,1408]{1,0:T(8,128)(2,1)S(1)}, bf16[3584,1408]{1,0:T(8,128)(2,1)}, u32[]{:S(2)}) copy-start(bf16[3584,1408]{1,0:T(8,128)(2,1)} %all-gather.2.cloned.1.call-done) | copy-start | bytes 30277636
  228.3 12.4 %collective-permute-start.5 = (bf16[256,896]{1,0:T(8,128)(2,1)S(1)}, bf16[256,896]{1,0:T(8,128)(2,1)S(1)}, u32[]{:S(2)}, u32[]{:S(2)}) collective-permute-start(bf16[256,896]{1,0:T(8,128)(2,1)S(1)} %fusion.36), channel_id=1, source_target_pairs={{0,2},{2,0},{1,3},{3,1},{4,6},{6,4},{5,7},{7,5},{8,10},{10,8},{9,1... | collective-permute-start | bytes 1376264 | tf_op jit(solution)/shard_map/ppermute | solution.py:116
  232.1 8.9 %copy-start.5 = (bf16[3584]{0:T(1024)(128)(2,1)S(1)}, bf16[3584]{0:T(1024)(128)(2,1)}, u32[]{:S(2)}) copy-start(bf16[3584]{0:T(1024)(128)(2,1)} %param.19) | copy-start | bytes 21508
  232.1 8.9 %copy-start.11 = (bf16[256]{0:T(256)(128)(2,1)S(1)}, bf16[256]{0:T(256)(128)(2,1)}, u32[]{:S(2)}) copy-start(bf16[256]{0:T(256)(128)(2,1)} %param.21) | copy-start | bytes 1540
  232.1 8.9 %copy-start.12 = (bf16[256]{0:T(256)(128)(2,1)S(1)}, bf16[256]{0:T(256)(128)(2,1)}, u32[]{:S(2)}) copy-start(bf16[256]{0:T(256)(128)(2,1)} %param.23) | copy-start | bytes 1540
  240.9 2.7 %collective-permute-start.6 = (bf16[256,1792]{1,0:T(8,128)(2,1)S(1)}, bf16[256,1792]{1,0:T(8,128)(2,1)}, u32[]{:S(2)}, u32[]{:S(2)}) collective-permute-start(bf16[256,1792]{1,0:T(8,128)(2,1)S(1)} %pad_maximum_fusion.10), channel_id=1, source_target_pairs={{0,1},{1,0},{2,3},{3,2},{4,5},{5,4},{6,7},{7,6},{8,9},{9,8},{10,11... | collective-permute-start | bytes 2752520 | tf_op jit(solution)/shard_map/ppermute | solution.py:39
Sparse Core Ops, SparseCore 0:
  27.7 194.9 all-gather.1

commit v4 on v3

--- a/solution.py
+++ b/solution.py
@@ -62,8 +62,8 @@
     w_value,
     b_value,
 ):
-    seq = ("o", "i")
-    seq_count = lax.axis_size("o") * lax.axis_size("i")
+    seq = ("o", "j", "i")
+    seq_count = lax.axis_size(seq)
     own_index = lax.axis_index(seq)
     pair_index = lax.axis_index("i")
     tok_rows = encoded.shape[0]
@@ -72,9 +72,16 @@
     rounds = tok_rows // round_span
     frames_here = frame_tokens.shape[1]
 
+    swap = [(0, 1), (1, 0)]
     out_rows = jnp.concatenate(swapped(w_out[:, :quarter], w_out[:, quarter:], "i"), axis=0)
+    in_rows = jnp.concatenate(swapped(w_in[:, :quarter], w_in[:, quarter:], "i"), axis=0)
+    all_in = lax.all_gather(jnp.concatenate(both(in_rows, "j")), "o", axis=0, tiled=True)
     kv_rows = jnp.concatenate(both(jnp.concatenate([w_key, w_value], axis=1), "i"), axis=0)
-    late = lax.all_gather(jnp.concatenate([out_rows, kv_rows], axis=1), "o", axis=0, tiled=True)
+    kv_rows = jnp.concatenate(both(kv_rows, "j"))
+    out_rows, kv_rows = lax.optimization_barrier((out_rows, kv_rows))
+    own_out = lax.all_gather(out_rows, "o", axis=0, tiled=True)
+    all_kv = lax.all_gather(kv_rows, "o", axis=0, tiled=True)
+    other_out = lax.ppermute(own_out, "j", swap)
 
     slot_order = jnp.argsort(slot_owner, stable=True)
     pick_rows = (
@@ -88,12 +95,6 @@
     arrived = lax.all_to_all(moved, seq, split_axis=0, concat_axis=0, tiled=True)
     all_counts = arrived[:, 0, encoded.shape[1] :][:, :frames_here].astype(jnp.int32)
     row_block = arrived[:, :, : encoded.shape[1]].reshape(tok_rows, encoded.shape[1])
-    parts = jnp.stack([w_in[:, :quarter], w_in[:, quarter:]])
-    parts = jnp.broadcast_to(parts[None], (lax.axis_size("o"),) + parts.shape)
-    all_in = lax.all_to_all(
-        parts.reshape(seq_count, -1, quarter), seq, split_axis=0, concat_axis=0, tiled=True
-    ).reshape(-1, quarter)
-    swap = [(0, 1), (1, 0)]
     first = pair_index == 0
     columns = jnp.concatenate([lax.ppermute(row_block, "i", swap), row_block], axis=0)
     own_b_in = lax.dynamic_slice_in_dim(b_in, pair_index * quarter, quarter)
@@ -109,12 +110,21 @@
     )
     hidden = jnp.concatenate(both(hidden, "mp"), axis=1)
 
-    def project(rows):
-        summed = jnp.dot(rows, late[:, :quarter], preferred_element_type=jnp.float32)
+    zeroth = lax.axis_index("j") == 0
+    units = hidden.reshape(hidden.shape[0], lax.axis_size("o"), PAIR, -1)
+    own_units = jnp.where(zeroth, units[:, :, 0], units[:, :, 1]).reshape(hidden.shape[0], -1)
+    other_units = jnp.where(zeroth, units[:, :, 1], units[:, :, 0]).reshape(hidden.shape[0], -1)
+    early = jnp.dot(own_units, own_out, preferred_element_type=jnp.float32)
+    early, other_out = lax.optimization_barrier((early, other_out))
+
+    def project(part):
+        summed = early[part] + jnp.dot(
+            other_units[part], other_out, preferred_element_type=jnp.float32
+        )
         return (summed + own_b_out.astype(jnp.float32)).astype(jnp.bfloat16)
 
-    got = lax.ppermute(project(hidden[:tok_rows]), "i", swap)
-    kept = project(hidden[tok_rows:])
+    got = lax.ppermute(project(slice(None, tok_rows)), "i", swap)
+    kept = project(slice(tok_rows, None))
     got, kept = lax.optimization_barrier((got, kept))
     projected = jnp.concatenate([jnp.where(first, kept, got), jnp.where(first, got, kept)], axis=1)
     wide = jnp.concatenate(both(projected, "mp"), axis=1).astype(jnp.float32)
@@ -134,7 +144,7 @@
 
     inv_rms = lax.rsqrt(jnp.mean(wide * wide, axis=1) + norm_eps)
     normed = (wide * inv_rms[:, None] * norm_gain.astype(jnp.float32)).astype(jnp.bfloat16)
-    linear = jnp.dot(normed, late[:, quarter:], preferred_element_type=jnp.float32)
+    linear = jnp.dot(normed, all_kv, preferred_element_type=jnp.float32)
     key_linear = linear[:, : w_key.shape[1]]
     value_linear = linear[:, w_key.shape[1] :]
     key_rows = rotate(key_linear + b_key.astype(jnp.float32), frame_ids, offsets).astype(
@@ -145,11 +155,11 @@
 
 
 def solution(mesh):
-    seq_count, mp_count = mesh.shape["seq"], mesh.shape["mp"]
+    mp_count = mesh.shape["mp"]
     paired = jax.sharding.Mesh(
-        mesh.devices.reshape(seq_count // PAIR, PAIR, mp_count), ("o", "i", "mp")
+        mesh.devices.reshape(-1, PAIR, PAIR, mp_count), ("o", "j", "i", "mp")
     )
-    seq = ("o", "i")
+    seq = ("o", "j", "i")
     return jax.shard_map(
         shards,
         mesh=paired,

time: 258 us -> 254 us (0.984)
  waiting for transfers between devices: 175 us -> 164 us
  other arithmetic: 15.9 us -> 23.6 us
  starting transfers between devices: 27.5 us -> 21 us
  local copies, waits for them, and re-layouts: 6.85 us -> 11.7 us
    ppermute x1 -> x2, waiting for transfers between devices: 8.58 us -> 63 us  [the longest x1 53.2 us: shards(): other_out = lax.ppermute(own_out, 'j', swap)]
    all_to_all x1 -> x0, waiting for transfers between devices: 35.6 us -> none  [shards(): lax.all_to_all(parts.reshape(seq_count, -1, quarter), seq, split_axis=0,...]
    all_to_all x1, waiting for transfers between devices: 27.6 us -> 3.22 us  [shards(): lax.all_to_all(moved, seq, split_axis=0, concat_axis=0, tiled=True)]
    all_to_all x1 -> x0, starting transfers between devices: 12.8 us -> none  [shards(): lax.all_to_all(parts.reshape(seq_count, -1, quarter), seq, split_axis=0,...]
    ppermute x1, waiting for transfers between devices: 15.7 us -> 9.24 us  [shards(): lax.ppermute(row_block, 'i', swap)]
    concatenate x0 -> x1, local copies, waits for them, and re-layouts: none -> 6.03 us  [shards(): hidden = jnp.concatenate(both(hidden, 'mp'), axis=1)]
    ppermute x3 -> x5, waiting for transfers between devices: 10.3 us -> 16 us  [both(): other = lax.ppermute(block, axis, [(0, 1), (1, 0)])]
    concatenate x1 -> x6, other arithmetic: 1.15 us -> 5.01 us  [the longest x1 2.09 us: shards(): hidden = jnp.concatenate(both(hidden, 'mp'), axis=1)]
  transfers between devices with their start and end apart: 10 -> 15, of which waited for: 10 -> 12; matrix products, arithmetic and copies ran while one was open for 9% -> 17% of each run, Pallas kernels for 0% -> 0%
where the time goes in v4:
time: 254 us
  waiting for transfers between devices  164 us (65%)
  other arithmetic  23.6 us (9%)
  starting transfers between devices  21 us (8%)
  matrix products  18.8 us (7%)
  between operations  14.2 us (6%)
  local copies, waits for them, and re-layouts  11.7 us (5%)
    ppermute x1, waiting for transfers between devices, shards(): other_out = lax.ppermute(own_out, 'j', swap)  53.2 us
    all_gather x1, waiting for transfers between devices, shards(): own_out = lax.all_gather(out_rows, 'o', axis=0, tiled=True)  33.6 us
    ppermute x1, waiting for transfers between devices, shards(): other = lax.ppermute(hidden, 'i', swap)  20.8 us
    ppermute x5, waiting for transfers between devices, both(): other = lax.ppermute(block, axis, [(0, 1), (1, 0)])  16 us
    all_gather x1, waiting for transfers between devices, shards(): lax.all_gather(jnp.concatenate(both(in_rows, 'j')), 'o', axis=0, tiled=True)  11.6 us
    ppermute x1, waiting for transfers between devices, shards(): got = lax.ppermute(project(slice(None, tok_rows)), 'i', swap)  9.77 us
    ppermute x1, waiting for transfers between devices, shards(): lax.ppermute(row_block, 'i', swap)  9.24 us
    dot_general x1, matrix products, shards(): pre = jnp.dot(columns, all_in, preferred_element_type=jnp.float32)  7.29 us
  transfers between devices with their start and end apart: 15, of which 12 were waited for; matrix products, arithmetic and copies ran while one was open for 17% of the time, Pallas kernels for 0%

profile of v4, /device:TPU:0, one launch (start us, length us, event | category | flops | bytes accessed | tf_op | source)
XLA Modules:
  0.0 253.6 jit_solution(15159665382444806847)
XLA Ops:
  7.2 1.0 broadcast_select_fusion.23
  8.3 3.0 %collective-permute-start.1 = (bf16[72,896]{1,0:T(8,128)(2,1)S(1)}, bf16[72,896]{1,0:T(8,128)(2,1)S(1)}, u32[]{:S(2)}, u32[]{:S(2)}) collective-permute-start(bf16[72,896]{1,0:T(8,128)(2,1)S(1)} %broadcast_select_fusion.23), channel_id=1, source_target_pairs={{0,2},{2,0},{1,3},{3,1},{4,6},{6,4},{5,7},{7,5},{8,10},{10,8},{9,1... | collective-permute-start | bytes 387080 | tf_op jit(solution)/shard_map/ppermute | solution.py:47
  11.3 2.3 sort.17
  13.6 0.1 copy.26
  13.8 0.1 add.174
  14.0 0.8 collective-permute-done.1
  14.8 1.0 broadcast_select_fusion.22
  15.8 1.8 collective-permute-start.2
  17.7 0.1 copy.21
  17.8 0.1 add.184
  17.9 5.3 %collective-permute-done.2 = bf16[144,896]{1,0:T(8,128)(2,1)S(1)} collective-permute-done((bf16[144,896]{1,0:T(8,128)(2,1)S(1)}, bf16[144,896]{1,0:T(8,128)(2,1)S(1)}, u32[]{:S(2)}, u32[]{:S(2)}) %collective-permute-start.2) | collective-permute-done | bytes 258080 | tf_op jit(solution)/shard_map/ppermute | solution.py:39
  23.2 0.1 broadcast_select_fusion.18
  23.3 0.9 pad_maximum_fusion.9
  24.2 1.3 gather_fusion
  25.6 0.1 broadcast_select_fusion.8
  25.7 0.9 pad_maximum_fusion.8
  26.7 6.8 %all-to-all-start = ((bf16[16,16,1280]{2,1,0:T(8,128)(2,1)}), bf16[16,16,1280]{2,1,0:T(8,128)(2,1)S(1)}, u32[]{:S(2)}, u32[]{:S(2)}) async-start(bf16[16,16,1280]{2,1,0:T(8,128)(2,1)} %pad_maximum_fusion.8), calls=%async_computation | async-start | bytes 1310720 | tf_op jit(solution)/shard_map/all_to_all | solution.py:95
  33.6 2.0 collective-permute-start.6
  35.7 0.2 collective-permute-start.5
  35.9 10.0 %collective-permute-done.6 = bf16[224,512]{1,0:T(8,128)(2,1)S(1)} collective-permute-done((bf16[224,512]{1,0:T(8,128)(2,1)S(1)}, bf16[224,512]{1,0:T(8,128)(2,1)S(1)}, u32[]{:S(2)}, u32[]{:S(2)}) %collective-permute-start.6) | collective-permute-done | bytes 229408 | tf_op jit(solution)/shard_map/ppermute | solution.py:39
  46.0 1.8 collective-permute-start.7
  47.7 6.0 %collective-permute-done.5 = bf16[224,896]{1,0:T(8,128)(2,1)S(1)} collective-permute-done((bf16[224,896]{1,0:T(8,128)(2,1)S(1)}, bf16[224,896]{1,0:T(8,128)(2,1)S(1)}, u32[]{:S(2)}, u32[]{:S(2)}) %collective-permute-start.5) | collective-permute-done | bytes 401440 | tf_op jit(solution)/shard_map/ppermute | solution.py:47
  53.7 0.1 broadcast_select_fusion.14
  53.8 1.0 pad_maximum_fusion.7
  54.8 0.7 collective-permute-done.7
  55.5 1.2 broadcast_select_fusion.10
  56.7 1.0 pad_maximum_fusion.5
  57.8 3.2 %all-to-all-done = bf16[16,16,1280]{2,1,0:T(8,128)(2,1)S(1)} async-done(((bf16[16,16,1280]{2,1,0:T(8,128)(2,1)}), bf16[16,16,1280]{2,1,0:T(8,128)(2,1)S(1)}, u32[]{:S(2)}, u32[]{:S(2)}) %all-to-all-start) | async-done | bytes 655392 | tf_op jit(solution)/shard_map/all_to_all | solution.py:95
  61.0 0.6 collective-permute-start
  61.8 9.2 %collective-permute-done = bf16[256,1152]{1,0:T(8,128)(2,1)S(1)} collective-permute-done((bf16[256,1152]{1,0:T(8,128)(2,1)S(1)}, bf16[256,1152]{1,0:T(8,128)(2,1)S(1)}, u32[]{:S(2)}, u32[]{:S(2)}) %collective-permute-start) | collective-permute-done | bytes 589856 | tf_op jit(solution)/shard_map/ppermute | solution.py:99
  71.0 11.6 %all-gather.4.cloned.1.call-done = bf16[1152,896]{1,0:T(8,128)(2,1)} async-done(((bf16[288,896]{1,0:T(8,128)(2,1)}), bf16[1152,896]{1,0:T(8,128)(2,1)}) %all-gather.4.cloned.1.call-update) | async-done | bytes 2064400 | tf_op jit(solution)/shard_map/all_gather | solution.py:78
  82.6 7.3 %fusion.5 = bf16[512,896]{1,0:T(8,128)(2,1)S(1)} fusion(bf16[1152,896]{1,0:T(8,128)(2,1)} %all-gather.4.cloned.1.call-done, bf16[256,1152]{1,0:T(8,128)(2,1)S(1)} %bitcast.31, bf16[256,1152]{1,0:T(8,128)(2,1)S(1)} %collective-permute-done, f32[896]{0:T(1024)S(1)} %dynamic-slice_convert_fusion.1), kind=kOutput, calls=%fused_computation.10 | convolution fusion | flops 1089601536 | bytes 4165120 | tf_op jit(solution)/shard_map/dot_general | solution.py:102
  89.9 1.5 collective-permute-start.3
  91.5 20.8 %collective-permute-done.3 = bf16[512,896]{1,0:T(8,128)(2,1)S(1)} collective-permute-done((bf16[512,896]{1,0:T(8,128)(2,1)S(1)}, bf16[512,896]{1,0:T(8,128)(2,1)S(1)}, u32[]{:S(2)}, u32[]{:S(2)}) %collective-permute-start.3) | collective-permute-done | bytes 917536 | tf_op jit(solution)/shard_map/ppermute | solution.py:106
  112.3 0.4 broadcast_select_fusion.5
  112.7 1.4 pad_maximum_fusion.1
  114.1 33.6 %all-gather.6.cloned.1.call-done = bf16[1792,896]{1,0:T(8,128)(2,1)} async-done(((bf16[448,896]{1,0:T(8,128)(2,1)}), bf16[1792,896]{1,0:T(8,128)(2,1)}) %all-gather.6.cloned.1.call-update) | async-done | bytes 3211280 | tf_op jit(solution)/shard_map/all_gather | solution.py:82
  147.7 1.5 collective-permute-start.8
  149.3 2.2 broadcast_select_fusion.1
  151.5 2.1 pad_maximum_fusion
  153.5 6.0 %copy.22 = bf16[512,3584]{0,1:T(8,128)(2,1)} copy(bf16[512,3584]{1,0:T(8,128)(2,1)} %pad_maximum_fusion) | data formatting | bytes 7340032 | tf_op jit(solution)/shard_map/concatenate | solution.py:111
  159.6 2.3 broadcast_select_fusion.3
  161.9 0.1 fusion.28
  162.0 1.8 copy-done.8
  163.8 2.1 fusion.30
  165.9 53.2 %collective-permute-done.8 = bf16[1792,896]{1,0:T(8,128)(2,1)} collective-permute-done((bf16[1792,896]{1,0:T(8,128)(2,1)}, bf16[1792,896]{1,0:T(8,128)(2,1)}, u32[]{:S(2)}, u32[]{:S(2)}) %collective-permute-start.8) | collective-permute-done | bytes 3211296 | tf_op jit(solution)/shard_map/ppermute | solution.py:84
  219.1 3.1 %fusion.31 = f32[256,896]{1,0:T(8,128)S(1)} fusion(bf16[256,1792]{0,1:T(8,128)(2,1)S(1)} %bitcast.29, bf16[1792,896]{1,0:T(8,128)(2,1)} %collective-permute-done.8), kind=kOutput, calls=%fused_computation.109 | convolution fusion | flops 822083584 | bytes 5046272 | tf_op jit(solution)/shard_map/dot_general | solution.py:121
  222.2 3.1 %add_convert_fusion = (bf16[256,896]{1,0:T(8,128)(2,1)S(1)}, bf16[256,896]{1,0:T(8,128)(2,1)S(1)}) fusion(f32[512,896]{1,0:T(8,128)S(1)} %fusion.30, f32[896]{0:T(1024)S(1)} %dynamic-slice_convert_fusion, f32[256,896]{1,0:T(8,128)S(1)} %fusion.31, bf16[256,1792]{0,1:T(8,128)(2,1)S(1)} %bitcast.28, bf16[1792,896]{1,0:T(8,128)(2,1)} %collective-permute-done.8), kind=kOutput, calls=%fused_computation.41 | convolution fusion | flops 823459840 | bytes 7802368 | tf_op jit(solution)/shard_map/dot_general | solution.py:121
  225.3 1.5 collective-permute-start.9
  226.9 9.8 %collective-permute-done.9 = bf16[256,896]{1,0:T(8,128)(2,1)S(1)} collective-permute-done((bf16[256,896]{1,0:T(8,128)(2,1)S(1)}, bf16[256,896]{1,0:T(8,128)(2,1)S(1)}, u32[]{:S(2)}, u32[]{:S(2)}) %collective-permute-start.9) | collective-permute-done | bytes 458784 | tf_op jit(solution)/shard_map/ppermute | solution.py:126
  236.6 0.1 broadcast_select_fusion.12
  236.9 0.4 copy-done.5
  237.5 0.1 add.204
  237.6 0.2 reduce_window_sum.11
  238.1 0.1 add.207
  238.2 1.2 fusion.22
  239.5 1.5 broadcast_select_fusion.7
  241.0 0.4 fusion
  241.5 3.2 %fusion.6 = f32[256,512]{1,0:T(8,128)S(1)} fusion(bf16[3584,512]{1,0:T(8,128)(2,1)} %all-gather.8.cloned.1.call-done, f32[3584]{0:T(1024)S(1)} %convert_element_type.77, f32[256]{0:T(256)S(1)} %add_rsqrt_fusion, bf16[256,1792]{1,0:T(8,128)(2,1)S(1)} %get-tuple-element.25, bf16[256,1792]{1,0:T(8,128)(2,1)S(1)} %get-tuple-element.24), kind=kOutput, calls=%fused_computation.11 | convolution fusion | flops 945946624 | bytes 6044672 | tf_op jit(solution)/shard_map/dot_general | solution.py:147
  244.7 0.7 fusion.20
  245.4 0.1 reshape.265
  245.5 0.5 subtract_convert_fusion
  246.0 0.4 pad_maximum_fusion.12
  246.4 0.7 copy.30
  (73 shorter events, 1.7 us)
Async XLA Ops:
  7.2 17.1 %copy-start = (bf16[256,1152]{1,0:T(8,128)(2,1)S(1)}, bf16[256,1152]{1,0:T(8,128)(2,1)}, u32[]{:S(2)}) copy-start(bf16[256,1152]{1,0:T(8,128)(2,1)} %param.12) | copy-start | bytes 1769476
  7.2 75.5 %all-gather.4.cloned.1.call-start = ((), (), s32[]{:S(2)}) async-start(), calls=%async_computation.1 | async-start | bytes 2580480 | tf_op jit(solution)/shard_map/all_gather | solution.py:78
  8.3 6.5 %collective-permute-start.1 = (bf16[72,896]{1,0:T(8,128)(2,1)S(1)}, bf16[72,896]{1,0:T(8,128)(2,1)S(1)}, u32[]{:S(2)}, u32[]{:S(2)}) collective-permute-start(bf16[72,896]{1,0:T(8,128)(2,1)S(1)} %broadcast_select_fusion.23), channel_id=1, source_target_pairs={{0,2},{2,0},{1,3},{3,1},{4,6},{6,4},{5,7},{7,5},{8,10},{10,8},{9,1... | collective-permute-start | bytes 387080 | tf_op jit(solution)/shard_map/ppermute | solution.py:47
  15.8 7.4 %collective-permute-start.2 = (bf16[144,896]{1,0:T(8,128)(2,1)S(1)}, bf16[144,896]{1,0:T(8,128)(2,1)S(1)}, u32[]{:S(2)}, u32[]{:S(2)}) collective-permute-start(bf16[144,896]{1,0:T(8,128)(2,1)S(1)} %pad_maximum_fusion.11), channel_id=1, source_target_pairs={{0,4},{4,0},{1,5},{5,1},{2,6},{6,2},{3,7},{7,3},{8,12},{12,8},{9,1... | collective-permute-start | bytes 774152 | tf_op jit(solution)/shard_map/ppermute | solution.py:39
  24.2 1.3 copy-start.9
  25.6 8.0 %copy-start.3 = (bf16[224,256]{1,0:T(8,128)(2,1)S(1)}, bf16[224,256]{1,0:T(8,128)(2,1)}, u32[]{:S(2)}) copy-start(bf16[224,256]{1,0:T(8,128)(2,1)} %param.20) | copy-start | bytes 344068
  25.6 8.0 %copy-start.4 = (bf16[224,256]{1,0:T(8,128)(2,1)S(1)}, bf16[224,256]{1,0:T(8,128)(2,1)}, u32[]{:S(2)}) copy-start(bf16[224,256]{1,0:T(8,128)(2,1)} %param.22) | copy-start | bytes 344068
  25.6 10.0 %copy-start.1 = (bf16[224,1792]{1,0:T(8,128)(2,1)S(1)}, bf16[224,1792]{1,0:T(8,128)(2,1)}, u32[]{:S(2)}) copy-start(bf16[224,1792]{1,0:T(8,128)(2,1)} %param.17) | copy-start | bytes 2408452
  26.7 34.3 %all-to-all-start = ((bf16[16,16,1280]{2,1,0:T(8,128)(2,1)}), bf16[16,16,1280]{2,1,0:T(8,128)(2,1)S(1)}, u32[]{:S(2)}, u32[]{:S(2)}) async-start(bf16[16,16,1280]{2,1,0:T(8,128)(2,1)} %pad_maximum_fusion.8), calls=%async_computation | async-start | bytes 1310720 | tf_op jit(solution)/shard_map/all_to_all | solution.py:95
  33.5 114.2 %all-gather.6.cloned.1.call-start = ((), (), s32[]{:S(2)}) async-start(), calls=%async_computation.2 | async-start | bytes 4014080 | tf_op jit(solution)/shard_map/all_gather | solution.py:82
  33.6 12.2 %collective-permute-start.6 = (bf16[224,512]{1,0:T(8,128)(2,1)S(1)}, bf16[224,512]{1,0:T(8,128)(2,1)S(1)}, u32[]{:S(2)}, u32[]{:S(2)}) collective-permute-start(bf16[224,512]{1,0:T(8,128)(2,1)S(1)} %constant_dynamic-update-slice_fusion), channel_id=1, source_target_pairs={{0,2},{2,0},{1,3},{3,1},{4,6},{6,4},{5,7},{7,5},{8,10},{10,8},{9,1... | collective-permute-start | bytes 688136 | tf_op jit(solution)/shard_map/ppermute | solution.py:39
  35.7 18.0 %collective-permute-start.5 = (bf16[224,896]{1,0:T(8,128)(2,1)S(1)}, bf16[224,896]{1,0:T(8,128)(2,1)S(1)}, u32[]{:S(2)}, u32[]{:S(2)}) collective-permute-start(bf16[224,896]{1,0:T(8,128)(2,1)S(1)} %broadcast_select_fusion.15), channel_id=1, source_target_pairs={{0,2},{2,0},{1,3},{3,1},{4,6},{6,4},{5,7},{7,5},{8,10},{10,8},{9,1... | collective-permute-start | bytes 1204232 | tf_op jit(solution)/shard_map/ppermute | solution.py:47
  46.0 9.5 %collective-permute-start.7 = (bf16[448,512]{1,0:T(8,128)(2,1)S(1)}, bf16[448,512]{1,0:T(8,128)(2,1)}, u32[]{:S(2)}, u32[]{:S(2)}) collective-permute-start(bf16[448,512]{1,0:T(8,128)(2,1)S(1)} %pad_maximum_fusion.10), channel_id=1, source_target_pairs={{0,4},{4,0},{1,5},{5,1},{2,6},{6,2},{3,7},{7,3},{8,12},{12,8},{9,1... | collective-permute-start | bytes 1376264 | tf_op jit(solution)/shard_map/ppermute | solution.py:39
  56.6 5.0 %copy-start.6 = (bf16[1792]{0:T(1024)(128)(2,1)S(1)}, bf16[1792]{0:T(1024)(128)(2,1)}, u32[]{:S(2)}) copy-start(bf16[1792]{0:T(1024)(128)(2,1)} %param.16) | copy-start | bytes 10756
  57.7 183.7 %all-gather.8.cloned.1.call-start = ((), (), s32[]{:S(2)}) async-start(), calls=%async_computation.3 | async-start | bytes 4587520 | tf_op jit(solution)/shard_map/all_gather | solution.py:83
  61.0 9.9 %collective-permute-start = (bf16[256,1152]{1,0:T(8,128)(2,1)S(1)}, bf16[256,1152]{1,0:T(8,128)(2,1)S(1)}, u32[]{:S(2)}, u32[]{:S(2)}) collective-permute-start(bf16[256,1152]{1,0:T(8,128)(2,1)S(1)} %bitcast.30), channel_id=1, source_target_pairs={{0,2},{2,0},{1,3},{3,1},{4,6},{6,4},{5,7},{7,5},{8,10},{10,8},{9,1... | collective-permute-start | bytes 1769480 | tf_op jit(solution)/shard_map/ppermute | solution.py:99
  89.9 22.3 %collective-permute-start.3 = (bf16[512,896]{1,0:T(8,128)(2,1)S(1)}, bf16[512,896]{1,0:T(8,128)(2,1)S(1)}, u32[]{:S(2)}, u32[]{:S(2)}) collective-permute-start(bf16[512,896]{1,0:T(8,128)(2,1)S(1)} %fusion.5), channel_id=1, source_target_pairs={{0,2},{2,0},{1,3},{3,1},{4,6},{6,4},{5,7},{7,5},{8,10},{10,8},{9,1... | collective-permute-start | bytes 2752520 | tf_op jit(solution)/shard_map/ppermute | solution.py:106
  112.7 36.5 %copy-start.7 = (bf16[1792]{0:T(1024)(128)(2,1)S(1)}, bf16[1792]{0:T(1024)(128)(2,1)}, u32[]{:S(2)}) copy-start(bf16[1792]{0:T(1024)(128)(2,1)} %param.18) | copy-start | bytes 10756
  114.1 35.2 %collective-permute-start.4 = (bf16[512,1792]{1,0:T(8,128)(2,1)}, bf16[512,1792]{1,0:T(8,128)(2,1)}, u32[]{:S(2)}, u32[]{:S(2)}) collective-permute-start(bf16[512,1792]{1,0:T(8,128)(2,1)} %pad_maximum_fusion.1), channel_id=1, source_target_pairs={{0,1},{1,0},{2,3},{3,2},{4,5},{5,4},{6,7},{7,6},{8,9},{9,8},{10,11... | collective-permute-start | bytes 5505032 | tf_op jit(solution)/shard_map/ppermute | solution.py:39
  147.7 71.4 %collective-permute-start.8 = (bf16[1792,896]{1,0:T(8,128)(2,1)}, bf16[1792,896]{1,0:T(8,128)(2,1)}, u32[]{:S(2)}, u32[]{:S(2)}) collective-permute-start(bf16[1792,896]{1,0:T(8,128)(2,1)} %all-gather.6.cloned.1.call-done), channel_id=1, source_target_pairs={{0,4},{4,0},{1,5},{5,1},{2,6},{6,2},{3,7},{7,3},{8,12},{12,8},{9,1... | collective-permute-start | bytes 9633800 | tf_op jit(solution)/shard_map/ppermute | solution.py:84
  161.9 1.9 copy-start.8
  225.3 11.3 %collective-permute-start.9 = (bf16[256,896]{1,0:T(8,128)(2,1)S(1)}, bf16[256,896]{1,0:T(8,128)(2,1)S(1)}, u32[]{:S(2)}, u32[]{:S(2)}) collective-permute-start(bf16[256,896]{1,0:T(8,128)(2,1)S(1)} %get-tuple-element.23), channel_id=1, source_target_pairs={{0,2},{2,0},{1,3},{3,1},{4,6},{6,4},{5,7},{7,5},{8,10},{10,8},{9,1... | collective-permute-start | bytes 1376264 | tf_op jit(solution)/shard_map/ppermute | solution.py:126
  236.6 0.7 copy-start.5
  236.6 0.7 copy-start.10
  236.6 0.7 copy-start.11
  236.8 2.7 %collective-permute-start.10 = (bf16[256,1792]{1,0:T(8,128)(2,1)S(1)}, bf16[256,1792]{1,0:T(8,128)(2,1)}, u32[]{:S(2)}, u32[]{:S(2)}) collective-permute-start(bf16[256,1792]{1,0:T(8,128)(2,1)S(1)} %pad_maximum_fusion.6), channel_id=1, source_target_pairs={{0,1},{1,0},{2,3},{3,2},{4,5},{5,4},{6,7},{7,6},{8,9},{9,8},{10,11... | collective-permute-start | bytes 2752520 | tf_op jit(solution)/shard_map/ppermute | solution.py:39
  241.4 4.1 %copy-start.2 = (f32[256,64]{1,0:T(8,128)S(1)}, f32[256,64]{1,0:T(8,128)}, u32[]{:S(2)}) copy-start(f32[256,64]{1,0:T(8,128)} %get-tuple-element.49) | copy-start | bytes 196612
Sparse Core Ops, SparseCore 0:
  24.3 58.2 all-gather.3
  84.2 63.4 all-gather.5
  149.4 70.5 all-gather.7
